TPU v7x, 128 devices: a whole 4x4x4 slice. The times are simulated.
128 devices in a mesh: energy: 32 (over y, x, core), mom: 4 (over z).
Axes of the slice: x: 4, y: 4, z: 4, core: 2. Of those that a mesh axis runs over, the one named last changes fastest.
Arguments:
- lesser: float32 [4, 32, 4, 4, 2, 128, 128], P(None, 'energy', 'mom'), as said below
- greater: float32 [4, 32, 4, 4, 2, 128, 128], P(None, 'energy', 'mom'), as said below
- hamiltonian: float32 [4, 4, 2, 128, 128], P('mom'), as said below
- coupling: float32 [4, 2, 128, 128], P('mom'), may hold values from -0.25 to 0.25
- shift: int32 [1], replicated, may hold values from 1 to 7
- phonon_weight: float32 [2], replicated, may hold values from 0.1 to 0.5
Outputs:
- lesser_next: float32 [4, 32, 4, 4, 2, 128, 128], P(None, 'energy', 'mom')
- greater_next: float32 [4, 32, 4, 4, 2, 128, 128], P(None, 'energy', 'mom')
- current: float32 [], replicated
Inputs may be any that keep to these rules, and one draw needn't show every extreme that they name: `lesser`: in each block the complex matrix is i times a Hermitian positive definite matrix. `greater`: in each block the complex matrix is -i times a Hermitian positive definite matrix. `hamiltonian`: each block is Hermitian: real part symmetric, imaginary part antisymmetric.
All inputs are finite; a program needn't handle non-finite values.
Results may differ from a plain program's by a relative error of at most 0.0001.
Values sent between devices are 32-bit elements; how exact they have to be, the bound alone decides.
A program may use at most 128 MiB of HBM per device.

v0:
```python
import jax
import jax.numpy as jnp
from jax import lax
from jax.sharding import Mesh
from jax.sharding import PartitionSpec as P

SMAX = 7
ENERGY = ("energy_0", "energy_1", "energy_2")
ENERGY_MOM = ("energy_0", "energy_1", "energy_2", "mom")


broaden = 0.2
contact_rate = 0.5
left_level = 0.3
right_level = -0.3
thermal = 0.1
band_edge = 2.0
precise = lax.Precision.HIGHEST


def shifted(array, axis, by):
    size = lax.axis_size(axis)
    return lax.ppermute(array, axis, [(i, (i + by) % size) for i in range(size)])


def in_blocks(array, dim, size):
    before, after = (array.shape[:dim], array.shape[dim + 1 :])
    return jnp.moveaxis(array.reshape(*before, size, -1, *after), dim, 0)


def summed_on_arrival(array, axis, dim):
    size = lax.axis_size(axis)
    blocks = lax.all_to_all(in_blocks(array, dim, size), axis, 0, 0, tiled=True)
    return jnp.sum(blocks, axis=0)


def by_axis(array, axes):
    for axis in axes:
        array = lax.psum(array, axis)
    return array


def product(left, right):
    return jnp.einsum("...ij,...jk->...ik", left, right, precision=precise)


def cmul(left, right):
    return (
        product(left[0], right[0]) - product(left[1], right[1]),
        product(left[0], right[1]) + product(left[1], right[0]),
    )


def dagger(value):
    return (jnp.swapaxes(value[0], -1, -2), -jnp.swapaxes(value[1], -1, -2))


def sandwich(outer, inner):
    return cmul(cmul(outer, inner), dagger(outer))


def invert(matrix):
    real, imag = matrix
    width = real.shape[-1]
    kernel = jnp.concatenate(
        [jnp.concatenate([real, -imag], -1), jnp.concatenate([imag, real], -1)], -2
    )
    normal = product(jnp.swapaxes(kernel, -1, -2), kernel)
    lower = jnp.linalg.cholesky(normal)
    rhs = jnp.concatenate([jnp.swapaxes(real, -1, -2), -jnp.swapaxes(imag, -1, -2)], -2)
    middle = jax.scipy.linalg.solve_triangular(lower, rhs, lower=True)
    result = jax.scipy.linalg.solve_triangular(lower, middle, lower=True, trans=1)
    guess = (result[..., :width, :], result[..., width:, :])
    check = cmul(matrix, guess)
    eye = jnp.eye(width, dtype=jnp.float32)
    return cmul(guess, (2.0 * eye - check[0], -check[1]))


def transport(energy, hamiltonian, coupling, sig_less, sig_great):
    slabs = hamiltonian.shape[1]
    width = hamiltonian.shape[-1]
    eye = jnp.eye(width, dtype=jnp.float32)
    level = energy[:, None, None]
    hop = (coupling[:, 0], coupling[:, 1])
    hop_back = dagger(hop)
    fill_left = jax.nn.sigmoid((left_level - energy) / thermal)
    fill_right = jax.nn.sigmoid((right_level - energy) / thermal)
    forward_r = []
    forward_l = []
    for slab in range(slabs):
        less_re = sig_less[:, slab, 0]
        less_im = sig_less[:, slab, 1]
        system_re = level * eye - hamiltonian[:, slab, 0] - 0.5 * (sig_great[:, slab, 0] - less_re)
        system_im = (
            broaden * eye - hamiltonian[:, slab, 1] - 0.5 * (sig_great[:, slab, 1] - less_im)
        )
        inject_re = less_re
        inject_im = less_im
        if slab == 0 or slab == slabs - 1:
            filling = fill_left if slab == 0 else fill_right
            system_im = system_im + contact_rate * eye
            inject_im = inject_im + 2.0 * contact_rate * filling[:, None, None] * eye
        if slab > 0:
            folded = sandwich(hop, forward_r[-1])
            system_re = system_re - folded[0]
            system_im = system_im - folded[1]
            carried = sandwich(hop, forward_l[-1])
            inject_re = inject_re + carried[0]
            inject_im = inject_im + carried[1]
        green = invert((system_re, system_im))
        forward_r.append(green)
        forward_l.append(sandwich(green, (inject_re, inject_im)))
    full_r = forward_r[-1]
    full_l = forward_l[-1]
    outs_r = [full_r]
    outs_l = [full_l]
    for slab in range(slabs - 2, -1, -1):
        green = forward_r[slab]
        green_l = forward_l[slab]
        lead = cmul(green, hop_back)
        spread = cmul(lead, full_r)
        tail = cmul(hop, green)
        extra = cmul(spread, tail)
        new_r = (green[0] + extra[0], green[1] + extra[1])
        cross = cmul(spread, cmul(hop, green_l))
        inner = sandwich(lead, full_l)
        cross_d = dagger(cross)
        new_l = (
            green_l[0] + inner[0] + cross[0] - cross_d[0],
            green_l[1] + inner[1] + cross[1] - cross_d[1],
        )
        full_r = new_r
        full_l = new_l
        outs_r.insert(0, full_r)
        outs_l.insert(0, full_l)
    less_blocks = jnp.stack([jnp.stack([value[0], value[1]], 1) for value in outs_l], 1)
    great_blocks = jnp.stack(
        [
            jnp.stack(
                [
                    outs_l[k][0] + outs_r[k][0] - jnp.swapaxes(outs_r[k][0], -1, -2),
                    outs_l[k][1] + outs_r[k][1] + jnp.swapaxes(outs_r[k][1], -1, -2),
                ],
                1,
            )
            for k in range(slabs)
        ],
        1,
    )
    great_trace = jnp.trace(great_blocks[:, 0, 1], axis1=-2, axis2=-1)
    less_trace = jnp.trace(less_blocks[:, 0, 1], axis1=-2, axis2=-1)
    flowing = -(
        2.0 * contact_rate * fill_left * great_trace
        + 2.0 * contact_rate * (1.0 - fill_left) * less_trace
    )
    return (less_blocks, great_blocks, flowing)


def displaced(field, amount):
    count = field.shape[1]
    padded = jnp.concatenate([jnp.zeros_like(field), field, jnp.zeros_like(field)], 1)
    start = count + jnp.clip(amount, -count, count)
    return lax.dynamic_slice_in_dim(padded, start, count, 1)


def onward(field, upward):
    blank = jnp.zeros_like(field[:, :1])
    if upward:
        return jnp.concatenate([field[:, 1:], blank], 1)
    return jnp.concatenate([blank, field[:, :-1]], 1)


def fetched(stacked, amount, upward):
    n_energy = lax.axis_size(ENERGY)
    here = lax.axis_index(ENERGY)
    whole_turns = amount // n_energy
    remainder = amount % n_energy
    direction = 1 if upward else -1
    stacked = displaced(stacked, direction * whole_turns)
    level = 1
    while level <= min(SMAX, n_energy - 1):
        if upward:
            arrived = shifted(stacked, ENERGY, -level)
            wrapped = here + level >= n_energy
        else:
            arrived = shifted(stacked, ENERGY, level)
            wrapped = here - level < 0
        arrived = jnp.where(wrapped, onward(arrived, upward), arrived)
        taken = remainder // level % 2 == 1
        stacked = jnp.where(taken, arrived, stacked)
        level = level * 2
    return stacked


def shards(lesser, greater, hamiltonian, coupling, shift, phonon_weight):
    n_energy = lax.axis_size(ENERGY)
    n_mom = lax.axis_size("mom")
    here = lax.axis_index(ENERGY)
    per_dev = lesser.shape[0]
    total = per_dev * n_energy
    both = jnp.stack([lesser[:, 0, 0], greater[:, 0, 0]], 0)
    amount = shift[0]
    emission = phonon_weight[0]
    absorption = phonon_weight[1]
    summed = summed_on_arrival(both, "mom", 2)
    mean = summed / n_mom
    upper = fetched(mean, amount, True)
    beneath = fetched(mean, amount, False)
    share_less = emission * upper[0] + absorption * beneath[0]
    share_great = emission * beneath[1] + absorption * upper[1]
    sig_both = lax.all_gather(jnp.stack([share_less, share_great], 0), "mom", axis=2, tiled=True)
    sig_less = sig_both[0]
    sig_great = sig_both[1]
    grid = (jnp.arange(per_dev) * n_energy + here).astype(jnp.float32)
    energy = (grid + 0.5) * (2.0 * band_edge / total) - band_edge
    ham_wide = jnp.broadcast_to(hamiltonian, (per_dev,) + hamiltonian.shape[1:])
    hop_wide = jnp.broadcast_to(coupling, (per_dev,) + coupling.shape[1:])
    less_new, great_new, flowing = transport(energy, ham_wide, hop_wide, sig_less, sig_great)
    partial_flow = jnp.sum(flowing) * (2.0 * band_edge / total)
    current = by_axis(partial_flow, ENERGY_MOM)
    return (less_new[:, None, None], great_new[:, None, None], current)


def solution(mesh):
    split = Mesh(
        mesh.devices.reshape(4, 4, 2, mesh.shape["mom"]),
        ("energy_0", "energy_1", "energy_2", "mom"),
    )
    return jax.shard_map(
        shards,
        mesh=split,
        in_specs=(
            P(None, ENERGY, "mom", None, None, None, None),
            P(None, ENERGY, "mom", None, None, None, None),
            P("mom", None, None, None, None),
            P("mom", None, None, None),
            P(),
            P(),
        ),
        out_specs=(
            P(None, ENERGY, "mom", None, None, None, None),
            P(None, ENERGY, "mom", None, None, None, None),
            P(),
        ),
        check_vma=False,
    )
```

profile of v0, /device:TPU:1, one launch (start us, length us, event | category | flops | bytes accessed | tf_op | source)
XLA Modules:
  0.0 1419.0 jit_solution(14913060354337525911)
XLA Ops:
  7.2 2.5 copy_bitcast_fusion
  9.7 2.3 maximum_bitcast_fusion
  11.9 5.8 all-to-all-start
  18.5 48.3 %all-to-all-done = f32[4,2,4,1,2,128,128]{6,5,4,2,1,3,0:T(8,128)} async-done(((f32[4,2,4,1,2,128,128]{6,5,4,2,1,3,0:T(8,128)}), f32[4,2,4,1,2,128,128]{6,5,4,2,1,3,0:T(8,128)}, u32[]{:S(2)}, u32[]{:S(2)}) %all-to-all-start) | async-done | bytes 4194336 | tf_op jit(solution)/shard_map/all_to_all | solution.py:33
  66.7 2.6 reduce_sum.34
  70.1 2.7 collective-permute-start.3
  72.8 11.7 collective-permute-done.3
  85.7 2.4 select_select_fusion.6
  91.9 3.6 collective-permute-start.1
  95.4 17.4 %collective-permute-done.4 = f32[2,4,1,2,128,128]{5,4,1,3,2,0:T(8,128)} collective-permute-done((f32[2,4,1,2,128,128]{5,4,1,3,2,0:T(8,128)}, f32[2,4,1,2,128,128]{5,4,1,3,2,0:T(8,128)}, u32[]{:S(2)}, u32[]{:S(2)}) %collective-permute-start.4) | collective-permute-done | bytes 1048608 | tf_op jit(solution)/shard_map/ppermute | solution.py:23
  119.3 3.0 collective-permute-start.2
  122.9 15.4 %collective-permute-done.5 = f32[2,4,1,2,128,128]{5,4,1,3,2,0:T(8,128)} collective-permute-done((f32[2,4,1,2,128,128]{5,4,1,3,2,0:T(8,128)S(1)}, f32[2,4,1,2,128,128]{5,4,1,3,2,0:T(8,128)}, u32[]{:S(2)}, u32[]{:S(2)}) %collective-permute-start.5) | collective-permute-done | bytes 1048608 | tf_op jit(solution)/shard_map/ppermute | solution.py:23
  139.4 13.6 collective-permute-done.2
  161.8 64.6 %all-gather.2.cloned.1.call-done = f32[2,4,4,2,128,128]{5,4,1,3,2,0:T(8,128)} async-done(((f32[2,4,1,2,128,128]{5,4,1,3,2,0:T(8,128)}), f32[2,4,4,2,128,128]{5,4,1,3,2,0:T(8,128)}) %all-gather.2.cloned.1.call-update) | async-done | bytes 4194320 | tf_op jit(solution)/shard_map/all_gather | solution.py:211
  226.4 2.5 slice_bitcast_fusion
  234.2 47.1 %custom-call.31 = f32[4,128,128]{2,1,0:T(8,128)S(1)} custom-call(f32[4,128,128]{2,1,0:T(8,128)S(1)} %cholesky.350), custom_call_target="Cholesky" | custom-call | tf_op jit(solution)/shard_map/jit(cholesky)/cholesky | solution.py:69
  281.4 39.3 %custom-call.32 = f32[4,1,128,128]{2,3,1,0:T(8,128)S(1)} custom-call(f32[4,1,128,128]{3,2,1,0:T(8,128)S(1)} %select_bitcast_fusion.3), custom_call_target="InvertDiagBlocksLowerTriangular" | custom-call | tf_op jit(solution)/shard_map/jit(cholesky)/cholesky | solution.py:69
  323.8 46.9 %custom-call.33 = f32[4,128,128]{2,1,0:T(8,128)S(1)} custom-call(f32[4,128,128]{2,1,0:T(8,128)S(1)} %convolution_subtract_fusion.57), custom_call_target="Cholesky" | custom-call | tf_op jit(solution)/shard_map/jit(cholesky)/cholesky | solution.py:69
  371.9 4.3 while.16
  376.8 79.0 %custom-call.35 = f32[4,2,128,128]{2,3,1,0:T(8,128)S(1)} custom-call(f32[4,2,128,128]{3,2,1,0:T(8,128)S(1)} %bitcast.802), custom_call_target="InvertDiagBlocksLowerTriangular" | custom-call | tf_op jit(solution)/shard_map/jit(_solve_triangular)/vmap()/triangular_solve | solution.py:72
  473.4 46.9 %custom-call.36 = f32[4,128,128]{2,1,0:T(8,128)S(1)} custom-call(f32[4,128,128]{2,1,0:T(8,128)S(1)} %cholesky.353), custom_call_target="Cholesky" | custom-call | tf_op jit(solution)/shard_map/jit(cholesky)/cholesky | solution.py:69
  521.1 39.3 %custom-call.37 = f32[4,1,128,128]{2,3,1,0:T(8,128)S(1)} custom-call(f32[4,1,128,128]{3,2,1,0:T(8,128)S(1)} %select_bitcast_fusion.2), custom_call_target="InvertDiagBlocksLowerTriangular" | custom-call | tf_op jit(solution)/shard_map/jit(cholesky)/cholesky | solution.py:69
  563.4 46.9 %custom-call.38 = f32[4,128,128]{2,1,0:T(8,128)S(1)} custom-call(f32[4,128,128]{2,1,0:T(8,128)S(1)} %convolution_subtract_fusion.47), custom_call_target="Cholesky" | custom-call | tf_op jit(solution)/shard_map/jit(cholesky)/cholesky | solution.py:69
  610.9 5.4 while.17
  617.0 79.8 %custom-call.40 = f32[4,2,128,128]{2,3,1,0:T(8,128)S(1)} custom-call(f32[4,2,128,128]{3,2,1,0:T(8,128)} %bitcast.803), custom_call_target="InvertDiagBlocksLowerTriangular" | custom-call | tf_op jit(solution)/shard_map/jit(_solve_triangular)/vmap()/triangular_solve | solution.py:72
  716.7 46.9 %custom-call.41 = f32[4,128,128]{2,1,0:T(8,128)S(1)} custom-call(f32[4,128,128]{2,1,0:T(8,128)S(1)} %cholesky.356), custom_call_target="Cholesky" | custom-call | tf_op jit(solution)/shard_map/jit(cholesky)/cholesky | solution.py:69
  764.5 40.7 %custom-call.42 = f32[4,1,128,128]{2,3,1,0:T(8,128)} custom-call(f32[4,1,128,128]{3,2,1,0:T(8,128)} %select_bitcast_fusion.1), custom_call_target="InvertDiagBlocksLowerTriangular" | custom-call | tf_op jit(solution)/shard_map/jit(cholesky)/cholesky | solution.py:69
  806.6 2.3 convolution_subtract_fusion.35
  808.9 48.3 %custom-call.43 = f32[4,128,128]{2,1,0:T(8,128)} custom-call(f32[4,128,128]{2,1,0:T(8,128)} %convolution_subtract_fusion.35), custom_call_target="Cholesky" | custom-call | tf_op jit(solution)/shard_map/jit(cholesky)/cholesky | solution.py:69
  861.5 5.4 while.18
  867.0 80.4 %custom-call.45 = f32[4,2,128,128]{2,3,1,0:T(8,128)} custom-call(f32[4,2,128,128]{3,2,1,0:T(8,128)} %bitcast.804), custom_call_target="InvertDiagBlocksLowerTriangular" | custom-call | tf_op jit(solution)/shard_map/jit(_solve_triangular)/vmap()/triangular_solve | solution.py:72
  963.4 3.0 fusion.62
  966.4 2.5 copy.409
  971.6 46.9 %custom-call.46 = f32[4,128,128]{2,1,0:T(8,128)S(1)} custom-call(f32[4,128,128]{2,1,0:T(8,128)S(1)} %cholesky.359), custom_call_target="Cholesky" | custom-call | tf_op jit(solution)/shard_map/jit(cholesky)/cholesky | solution.py:69
  1021.0 40.7 %custom-call.47 = f32[4,1,128,128]{2,3,1,0:T(8,128)} custom-call(f32[4,1,128,128]{3,2,1,0:T(8,128)} %select_bitcast_fusion), custom_call_target="InvertDiagBlocksLowerTriangular" | custom-call | tf_op jit(solution)/shard_map/jit(cholesky)/cholesky | solution.py:69
  1063.2 2.3 convolution_subtract_fusion.23
  1065.5 48.4 %custom-call.48 = f32[4,128,128]{2,1,0:T(8,128)} custom-call(f32[4,128,128]{2,1,0:T(8,128)} %convolution_subtract_fusion.23), custom_call_target="Cholesky" | custom-call | tf_op jit(solution)/shard_map/jit(cholesky)/cholesky | solution.py:69
  1118.2 5.4 while.19
  1123.6 80.4 %custom-call.50 = f32[4,2,128,128]{2,3,1,0:T(8,128)} custom-call(f32[4,2,128,128]{3,2,1,0:T(8,128)} %bitcast.801), custom_call_target="InvertDiagBlocksLowerTriangular" | custom-call | tf_op jit(solution)/shard_map/jit(_solve_triangular)/vmap()/triangular_solve | solution.py:72
  1268.5 2.4 fusion.8
  1277.6 2.6 fusion.281
  1310.3 2.6 fusion.280
  1344.3 2.4 fusion
  1352.3 2.6 fusion.37
  1375.6 9.1 psum.28
  1384.8 9.0 psum.29
  1394.0 7.6 psum.30
  1404.7 7.2 psum.31
  (614 shorter events, 288.3 us)
Async XLA Ops:
  11.9 54.8 %all-to-all-start = ((f32[4,2,4,1,2,128,128]{6,5,4,2,1,3,0:T(8,128)}), f32[4,2,4,1,2,128,128]{6,5,4,2,1,3,0:T(8,128)}, u32[]{:S(2)}, u32[]{:S(2)}) async-start(f32[4,2,4,1,2,128,128]{6,5,4,2,1,3,0:T(8,128)} %maximum_bitcast_fusion), calls=%async_computation | async-start | bytes 8388608 | tf_op jit(solution)/shard_map/all_to_all | solution.py:33
  17.8 208.6 %all-gather.2.cloned.1.call-start = ((), (), s32[]{:S(2)}) async-start(), calls=%async_computation.1 | async-start | bytes 5242880 | tf_op jit(solution)/shard_map/all_gather | solution.py:211
  70.1 14.4 %collective-permute-start.3 = (f32[2,4,1,2,128,128]{5,4,1,3,2,0:T(8,128)S(1)}, f32[2,4,1,2,128,128]{5,4,1,3,2,0:T(8,128)}, u32[]{:S(2)}, u32[]{:S(2)}) collective-permute-start(f32[2,4,1,2,128,128]{5,4,1,3,2,0:T(8,128)S(1)} %get-tuple-element.138), channel_id=1, source_target_pairs={{0,4},{4,8},{8,12},{12,16},{16,20},{20,24},{24,28},{28,32},{32,36}... | collective-permute-start | bytes 3145736 | tf_op jit(solution)/shard_map/ppermute | solution.py:23
  72.8 16.5 %collective-permute-start = (f32[2,4,1,2,128,128]{5,4,1,3,2,0:T(8,128)S(1)}, f32[2,4,1,2,128,128]{5,4,1,3,2,0:T(8,128)}, u32[]{:S(2)}, u32[]{:S(2)}) collective-permute-start(f32[2,4,1,2,128,128]{5,4,1,3,2,0:T(8,128)S(1)} %get-tuple-element.139), channel_id=1, source_target_pairs={{0,124},{4,0},{8,4},{12,8},{16,12},{20,16},{24,20},{28,24},{32,28}... | collective-permute-start | bytes 3145736 | tf_op jit(solution)/shard_map/ppermute | solution.py:23
  88.1 24.8 %collective-permute-start.4 = (f32[2,4,1,2,128,128]{5,4,1,3,2,0:T(8,128)}, f32[2,4,1,2,128,128]{5,4,1,3,2,0:T(8,128)}, u32[]{:S(2)}, u32[]{:S(2)}) collective-permute-start(f32[2,4,1,2,128,128]{5,4,1,3,2,0:T(8,128)} %select_select_fusion.6), channel_id=1, source_target_pairs={{0,8},{4,12},{8,16},{12,20},{16,24},{20,28},{24,32},{28,36},{32,40... | collective-permute-start | bytes 3145736 | tf_op jit(solution)/shard_map/ppermute | solution.py:23
  91.8 22.3 %copy-start.37 = (f32[2,4,1,2,128,128]{5,4,1,3,2,0:T(8,128)}, f32[2,4,1,2,128,128]{5,4,1,3,2,0:T(8,128)S(1)}, u32[]{:S(2)}) copy-start(f32[2,4,1,2,128,128]{5,4,1,3,2,0:T(8,128)S(1)} %select_select_fusion.9) | copy-start | bytes 3145732
  91.9 24.6 %collective-permute-start.1 = (f32[2,4,1,2,128,128]{5,4,1,3,2,0:T(8,128)S(1)}, f32[2,4,1,2,128,128]{5,4,1,3,2,0:T(8,128)}, u32[]{:S(2)}, u32[]{:S(2)}) collective-permute-start(f32[2,4,1,2,128,128]{5,4,1,3,2,0:T(8,128)S(1)} %select_select_fusion.9), channel_id=1, source_target_pairs={{0,120},{4,124},{8,0},{12,4},{16,8},{20,12},{24,16},{28,20},{32,24... | collective-permute-start | bytes 3145736 | tf_op jit(solution)/shard_map/ppermute | solution.py:23
  114.2 24.1 %collective-permute-start.5 = (f32[2,4,1,2,128,128]{5,4,1,3,2,0:T(8,128)S(1)}, f32[2,4,1,2,128,128]{5,4,1,3,2,0:T(8,128)}, u32[]{:S(2)}, u32[]{:S(2)}) collective-permute-start(f32[2,4,1,2,128,128]{5,4,1,3,2,0:T(8,128)S(1)} %select_select_fusion.5), channel_id=1, source_target_pairs={{0,16},{4,20},{8,24},{12,28},{16,32},{20,36},{24,40},{28,44},{32,4... | collective-permute-start | bytes 3145736 | tf_op jit(solution)/shard_map/ppermute | solution.py:23
  119.3 33.7 %collective-permute-start.2 = (f32[2,4,1,2,128,128]{5,4,1,3,2,0:T(8,128)S(1)}, f32[2,4,1,2,128,128]{5,4,1,3,2,0:T(8,128)}, u32[]{:S(2)}, u32[]{:S(2)}) collective-permute-start(f32[2,4,1,2,128,128]{5,4,1,3,2,0:T(8,128)S(1)} %select_select_fusion.8), channel_id=1, source_target_pairs={{0,112},{4,116},{8,120},{12,124},{16,0},{20,4},{24,8},{28,12},{32,... | collective-permute-start | bytes 3145736 | tf_op jit(solution)/shard_map/ppermute | solution.py:23
  159.1 69.8 %copy-start.117 = (f32[4]{0:T(128)}, f32[4]{0:T(128)S(1)}, u32[]{:S(2)}) copy-start(f32[4]{0:T(128)S(1)} %multiply_add_fusion.3) | copy-start | bytes 52
  160.3 121.1 %copy-start.106 = (pred[128,128]{1,0:T(8,128)(4,1)}, pred[128,128]{1,0:T(8,128)(4,1)S(1)}, u32[]{:S(2)}) copy-start(pred[128,128]{1,0:T(8,128)(4,1)S(1)} %iota_compare_fusion.1) | copy-start | bytes 49156
  161.8 67.1 %copy-start.102 = (f32[128,128]{1,0:T(8,128)}, f32[128,128]{1,0:T(8,128)S(1)}, u32[]{:S(2)}) copy-start(f32[128,128]{1,0:T(8,128)S(1)} %get-tuple-element.184) | copy-start | bytes 196612
  610.8 86.7 %copy-start.62 = (f32[4,128,128]{2,1,0:T(8,128)S(1)}, f32[4,128,128]{2,1,0:T(8,128)}, u32[]{:S(2)}) copy-start(f32[4,128,128]{2,1,0:T(8,128)} %copy-done.61) | copy-start | bytes 786436
  714.4 49.3 %copy-start.107 = (pred[128,128]{1,0:T(8,128)(4,1)S(1)}, pred[128,128]{1,0:T(8,128)(4,1)}, u32[]{:S(2)}) copy-start(pred[128,128]{1,0:T(8,128)(4,1)} %copy-done.106) | copy-start | bytes 49156
  960.0 6.4 copy-start.16
  969.0 50.3 %copy-start.108 = (pred[128,128]{1,0:T(8,128)(4,1)S(1)}, pred[128,128]{1,0:T(8,128)(4,1)}, u32[]{:S(2)}) copy-start(pred[128,128]{1,0:T(8,128)(4,1)} %copy-done.106) | copy-start | bytes 49156
  1233.6 6.9 copy-start.59
  1241.1 7.9 copy-start.25
  1256.4 7.1 copy-start.50
  1280.3 5.6 copy-start.41
  1281.3 5.9 copy-start.26
  1281.3 5.9 copy-start.34
  1281.4 5.9 copy-start.92
  1281.8 6.8 copy-start.60
  1281.8 6.8 copy-start.76
  1281.8 6.8 copy-start.94
  1293.7 6.8 copy-start.63
  1294.1 5.7 copy-start.30
  1294.1 5.7 copy-start.96
  1305.6 7.4 copy-start.27
  1312.9 5.7 copy-start.43
  1312.9 5.7 copy-start.15
  1314.0 6.0 copy-start.21
  1314.0 6.0 copy-start.32
  1314.0 6.0 copy-start.89
  1314.4 6.9 copy-start.56
  1314.5 6.9 copy-start.74
  1314.5 6.9 copy-start.93
  1327.2 7.9 copy-start.48
  1344.3 7.9 copy-start.54
  1350.1 6.6 copy-start.83
  1352.3 7.6 copy-start.52
  1359.9 6.2 copy-start.84
  1373.7 10.9 copy-start.97
  1373.8 20.1 %copy-start.98 = (f32[4,1,128,128]{3,2,0,1:T(8,128)S(1)}, f32[4,1,128,128]{3,2,0,1:T(8,128)}, u32[]{:S(2)}) copy-start(f32[4,1,128,128]{3,2,0,1:T(8,128)} %get-tuple-element.117) | copy-start | bytes 786436
  1373.8 27.9 %copy-start.88 = (f32[4,1,128,128]{2,3,0,1:T(8,128)S(1)}, f32[4,1,128,128]{2,3,0,1:T(8,128)}, u32[]{:S(2)}) copy-start(f32[4,1,128,128]{2,3,0,1:T(8,128)} %fusion.115) | copy-start | bytes 786436
  1375.6 27.0 %copy-start.90 = (f32[4,1,128,128]{2,3,0,1:T(8,128)S(1)}, f32[4,1,128,128]{2,3,0,1:T(8,128)}, u32[]{:S(2)}) copy-start(f32[4,1,128,128]{2,3,0,1:T(8,128)} %fusion.116) | copy-start | bytes 786436
  1375.6 27.1 %copy-start.91 = (f32[4,1,128,128]{2,3,0,1:T(8,128)S(1)}, f32[4,1,128,128]{2,3,0,1:T(8,128)}, u32[]{:S(2)}) copy-start(f32[4,1,128,128]{2,3,0,1:T(8,128)} %fusion.118) | copy-start | bytes 786436
  (87 other events, 276.9 us)
Sparse Core Ops, SparseCore 0:
  158.5 67.8 all-gather.1
where the time goes:
time: 1430 us; the launch traced here: 1420 us
  other arithmetic  905 us (63%)
  matrix products  189 us (13%)
  waiting for transfers between devices  171 us (12%)
  local copies, waits for them, and re-layouts  83.7 us (6%)
  blocking collectives  33 us (2%)
  between operations  18.7 us (1%)
  starting transfers between devices  18.5 us (1%)
    another operation x34, other arithmetic, invert(): lower = jnp.linalg.cholesky(normal)  544 us
    another operation x10, other arithmetic, invert(): jax.scipy.linalg.solve_triangular(lower, middle, lower=True, trans=1)  323 us
    dot_general x188, matrix products, product(): return jnp.einsum('...ij,...jk->...ik', left, right, precision=precise)  158 us
    all_gather x1, waiting for transfers between devices, shards(): lax.all_gather(jnp.stack([share_less, share_great], 0), 'mom', axis=2, ti...  64.6 us
    ppermute x6, waiting for transfers between devices, shifted(): lax.ppermute(array, axis, [(i, (i + by) % size) for i in range(size)])  58.1 us
    all_to_all x1, waiting for transfers between devices, summed_on_arrival(): blocks = lax.all_to_all(in_blocks(array, dim, size), axis, 0, 0, tiled=True)  48.3 us
    psum x4, blocking collectives, by_axis(): array = lax.psum(array, axis)  33 us
  transfers between devices with their start and end apart: 8, of which 6 were waited for; matrix products, arithmetic and copies ran while one was open for 1% of the time, Pallas kernels for 0%

commit v1 on v0

v1 whole, which is shorter than its diff:
```python
import functools

import jax
import jax.numpy as jnp
from jax import lax
from jax.experimental import pallas as pl
from jax.experimental.pallas import tpu as pltpu
from jax.sharding import PartitionSpec as P

SMAX = 7
broaden = 0.2
contact_rate = 0.5
left_level = 0.3
right_level = -0.3
thermal = 0.1
band_edge = 2.0

W = 128
BF = jnp.bfloat16
F32 = jnp.float32
LEAST = 0.03


def store(ref, real, imag):
    for row, part in ((0, real), (W, imag)):
        high = part.astype(BF)
        ref[row : row + W, :W] = high
        ref[row : row + W, W:] = (part - high.astype(F32)).astype(BF)


def store_high(ref, real, imag):
    ref[:W, :W] = real.astype(BF)
    ref[W:, :W] = imag.astype(BF)


def product(left, right, dagger=False, high=False):
    if high:
        lhs = left[:, :W]
    else:
        whole = left[...]
        lhs = jnp.concatenate([whole, whole], 1)
    if dagger:
        up = right[:, :W]
        low = None if high else right[:, W:]
        rhs = up if high else jnp.concatenate([up, up, low, low], 1)
        dims = (((1,), (1,)), ((), ()))
    else:
        up = jnp.concatenate([right[:W, :W], right[W:, :W]], 1)
        if high:
            rhs = up
        else:
            low = jnp.concatenate([right[:W, W:], right[W:, W:]], 1)
            rhs = jnp.concatenate([up, up, low, low], 0)
        dims = (((1,), (0,)), ((), ()))
    full = lax.dot_general(lhs, rhs, dims, preferred_element_type=F32)
    if dagger:
        return full[:W, :W] + full[W:, W:], full[W:, :W] - full[:W, W:]
    return full[:W, :W] - full[W:, W:], full[:W, W:] + full[W:, :W]


def kernel(
    where_ref, scal_ref, sig_ref, ham_ref, hop_ref,
    less_ref, great_ref, flow_ref,
    hop_f, sys_f, inv_f, tmp_f, inj_f, gr_f, t_f, l_f, full_f,
    inv, gl, gr, folded_r, folded_l,
):
    count = sig_ref.shape[2]
    slabs = ham_ref.shape[0]
    energies = range(count)
    rows = lax.broadcasted_iota(jnp.int32, (W, W), 0)
    cols = lax.broadcasted_iota(jnp.int32, (W, W), 1)
    eye = jnp.where(rows == cols, 1.0, 0.0).astype(F32)
    here = where_ref[0]

    def unpack(value):
        turned = value.T
        real = jnp.where(rows < cols, value, jnp.where(rows > cols, -turned, 0.0))
        imag = jnp.where(rows >= cols, value, turned)
        return real, imag

    store(hop_f, hop_ref[0].T, -hop_ref[1].T)

    def forward(slab, last):
        place = lax.rem(slab - here + slabs, slabs)
        at_left = jnp.where(slab == 0, 1.0, 0.0)
        norms = []
        for e in energies:
            less = unpack(sig_ref[place, 0, e])
            great = unpack(sig_ref[place, 1, e])
            fill = scal_ref[2, e] if last else at_left * scal_ref[1, e]
            contact = contact_rate if last else at_left * contact_rate
            sys_r = scal_ref[0, e] * eye - ham_ref[slab, 0] - 0.5 * (great[0] - less[0])
            sys_i = (broaden + contact) * eye - ham_ref[slab, 1] - 0.5 * (great[1] - less[1])
            inj_r = less[0]
            inj_i = less[1] + 2.0 * contact_rate * fill * eye
            if not last:
                sys_r = sys_r - folded_r[e, 0]
                sys_i = sys_i - folded_r[e, 1]
                inj_r = inj_r + folded_l[e, 0]
                inj_i = inj_i + folded_l[e, 1]
            store(sys_f.at[e], sys_r, sys_i)
            store(inj_f.at[e], inj_r, inj_i)
            back_r = sys_r.T
            back_i = -sys_i.T
            inv[e, 0] = back_r
            inv[e, 1] = back_i
            store_high(inv_f.at[e], back_r, back_i)
        for e in energies:
            real, imag = product(inv_f.at[e], sys_f.at[e], high=True)
            norms.append(jnp.sum(jnp.sqrt(real * real + imag * imag), axis=0, keepdims=True))
        bound = functools.reduce(jnp.maximum, norms)
        bound = 1.05 * jnp.max(bound)
        scale = 1.0 / bound
        for e in energies:
            real = inv[e, 0] * scale
            imag = inv[e, 1] * scale
            inv[e, 0] = real
            inv[e, 1] = imag
            store_high(inv_f.at[e], real, imag)

        def grow(carry):
            lowest, done = carry
            used = jnp.maximum(lowest, LEAST)
            a = 4.0 / (1.0 + used)
            b = a / (1.0 + used)
            after = jnp.minimum(lowest * (a - b * lowest), b * used)
            centre = jnp.where(after >= 0.9, 2.0 / (1.0 + after), 1.0)
            for e in energies:
                real, imag = product(inv_f.at[e], sys_f.at[e], high=True)
                store_high(tmp_f.at[e], real, imag)
            for e in energies:
                real, imag = product(tmp_f.at[e], inv_f.at[e], high=True)
                real = centre * (a * inv[e, 0] - b * real)
                imag = centre * (a * inv[e, 1] - b * imag)
                inv[e, 0] = real
                inv[e, 1] = imag
                store_high(inv_f.at[e], real, imag)
            return after, done + 1

        lax.while_loop(
            lambda carry: jnp.logical_and(carry[0] < 0.9, carry[1] < 64),
            grow,
            (broaden * broaden * scale, jnp.int32(0)),
        )
        for e in energies:
            store(inv_f.at[e], inv[e, 0], inv[e, 1])

        def refine(carry):
            sizes = []
            for e in energies:
                real, imag = product(inv_f.at[e], sys_f.at[e])
                real = eye - real
                sizes.append(jnp.sum(real * real + imag * imag, axis=0, keepdims=True))
                store_high(tmp_f.at[e], real, -imag)
            for e in energies:
                real, imag = product(tmp_f.at[e], inv_f.at[e], high=True)
                real = inv[e, 0] + real
                imag = inv[e, 1] + imag
                inv[e, 0] = real
                inv[e, 1] = imag
                store(inv_f.at[e], real, imag)
            return jnp.max(functools.reduce(jnp.maximum, [jnp.sum(size) for size in sizes])), carry[1] + 1

        lax.while_loop(
            lambda carry: jnp.logical_and(carry[0] > 4.0e-6, carry[1] < 24),
            refine,
            (jnp.float32(1.0), jnp.int32(0)),
        )
        for e in energies:
            gr[slab, e, 0] = inv[e, 0]
            gr[slab, e, 1] = inv[e, 1]
            store(gr_f.at[slab, e], inv[e, 0], inv[e, 1])
            real, imag = product(inv_f.at[e], inj_f.at[e])
            store(tmp_f.at[e], real, imag)
        for e in energies:
            real, imag = product(tmp_f.at[e], inv_f.at[e], dagger=True)
            gl[slab, e, 0] = real
            gl[slab, e, 1] = imag
            store(inj_f.at[e], real, imag)

    def fold(slab):
        for e in energies:
            real, imag = product(hop_f, gr_f.at[slab, e])
            store(t_f.at[slab, e], real, imag)
            real, imag = product(hop_f, inj_f.at[e])
            store(l_f.at[slab, e], real, imag)
        for e in energies:
            real, imag = product(t_f.at[slab, e], hop_f, dagger=True)
            folded_r[e, 0] = real
            folded_r[e, 1] = imag
            real, imag = product(l_f.at[slab, e], hop_f, dagger=True)
            folded_l[e, 0] = real
            folded_l[e, 1] = imag

    forward(slabs - 1, True)

    def down(step, carry):
        slab = slabs - 2 - step
        fold(slab + 1)
        forward(slab, False)
        return carry

    lax.fori_loop(0, slabs - 1, down, 0)

    def finish(slab, e, green, less):
        less_ref[e, slab, 0] = less[0]
        less_ref[e, slab, 1] = less[1]
        great_r = less[0] + green[0] - green[0].T
        great_i = less[1] + green[1] + green[1].T
        great_ref[e, slab, 0] = great_r
        great_ref[e, slab, 1] = great_i
        return great_i

    flow = jnp.zeros((1, W), F32)
    for e in energies:
        green = (gr[0, e, 0], gr[0, e, 1])
        less = (gl[0, e, 0], gl[0, e, 1])
        great_i = finish(0, e, green, less)
        fill = scal_ref[1, e]
        mixed = fill * great_i + (1.0 - fill) * less[1]
        flow = flow - jnp.sum(jnp.where(rows == cols, mixed, 0.0), axis=0, keepdims=True)
        store(full_f.at[0, e], *green)
        store(full_f.at[1, e], *less)
    flow_ref[...] = jnp.broadcast_to(jnp.sum(flow, axis=1, keepdims=True), flow_ref.shape)

    def up(slab, carry):
        for e in energies:
            real, imag = product(gr_f.at[slab, e], hop_f, dagger=True)
            store(sys_f.at[e], real, imag)
        for e in energies:
            real, imag = product(sys_f.at[e], full_f.at[0, e])
            store(tmp_f.at[e], real, imag)
            real, imag = product(sys_f.at[e], full_f.at[1, e])
            store(inj_f.at[e], real, imag)
        for e in energies:
            real, imag = product(tmp_f.at[e], t_f.at[slab, e])
            green = (gr[slab, e, 0] + real, gr[slab, e, 1] + imag)
            cross = product(tmp_f.at[e], l_f.at[slab, e])
            real, imag = product(inj_f.at[e], sys_f.at[e], dagger=True)
            less = (
                gl[slab, e, 0] + real + cross[0] - cross[0].T,
                gl[slab, e, 1] + imag + cross[1] + cross[1].T,
            )
            finish(slab, e, green, less)
            store(full_f.at[0, e], *green)
            store(full_f.at[1, e], *less)
        return carry

    lax.fori_loop(1, slabs, up, 0)


def transport(place, scalars, sigma, hamiltonian, coupling):
    slabs, _, count = sigma.shape[:3]
    form = (2 * W, 2 * W)
    vmem = pl.BlockSpec(memory_space=pltpu.VMEM)
    smem = pl.BlockSpec(memory_space=pltpu.SMEM)
    blocks = jax.ShapeDtypeStruct((count, slabs, 2, W, W), F32)
    return pl.pallas_call(
        kernel,
        out_shape=(blocks, blocks, jax.ShapeDtypeStruct((8, W), F32)),
        in_specs=[smem, smem, vmem, vmem, vmem],
        out_specs=(vmem, vmem, vmem),
        scratch_shapes=[
            pltpu.VMEM(form, BF),
            pltpu.VMEM((count,) + form, BF),
            pltpu.VMEM((count,) + form, BF),
            pltpu.VMEM((count,) + form, BF),
            pltpu.VMEM((count,) + form, BF),
            pltpu.VMEM((slabs, count) + form, BF),
            pltpu.VMEM((slabs, count) + form, BF),
            pltpu.VMEM((slabs, count) + form, BF),
            pltpu.VMEM((2, count) + form, BF),
            pltpu.VMEM((count, 2, W, W), F32),
            pltpu.VMEM((slabs, count, 2, W, W), F32),
            pltpu.VMEM((slabs, count, 2, W, W), F32),
            pltpu.VMEM((count, 2, W, W), F32),
            pltpu.VMEM((count, 2, W, W), F32),
        ],
        compiler_params=pltpu.CompilerParams(vmem_limit_bytes=48 * 1024 * 1024),
        cost_estimate=pl.CostEstimate(flops=20_000_000_000, bytes_accessed=8_000_000, transcendentals=0),
    )(place, scalars, sigma, hamiltonian, coupling)


def moved(array, axis, by):
    size = lax.axis_size(axis)
    return lax.ppermute(array, axis, [(i, (i + by) % size) for i in range(size)])


def block(array, index):
    return lax.dynamic_index_in_dim(array, index, 0, keepdims=False)


def onward(field, upward):
    blank = jnp.zeros_like(field[:1])
    if upward:
        return jnp.concatenate([field[1:], blank], 0)
    return jnp.concatenate([blank, field[:-1]], 0)


def shards(lesser, greater, hamiltonian, coupling, shift, phonon_weight):
    n_energy = lax.axis_size("energy")
    n_mom = lax.axis_size("mom")
    here = lax.axis_index("energy")
    me = lax.axis_index("mom")
    count = lesser.shape[0]
    total = count * n_energy
    upper = jnp.triu(jnp.ones((W, W), jnp.bool_), 1)

    def packed(field):
        field = field[:, 0, 0]
        return jnp.swapaxes(jnp.where(upper, field[:, :, 0], field[:, :, 1]), 0, 1)

    less = packed(lesser)
    great = packed(greater)
    after, before, across = (me + 1) % n_mom, (me + n_mom - 1) % n_mom, (me + 2) % n_mom
    first_a = moved(block(less, across), "mom", 1)
    first_b = moved(block(great, across), "mom", -1)
    second_a = moved(jnp.stack([block(less, after) + first_a, block(great, after)]), "mom", 1)
    second_b = moved(jnp.stack([block(less, before), block(great, before) + first_b]), "mom", -1)
    summed = jnp.stack([block(less, me), block(great, me)]) + (second_a + second_b)

    def exchange(by):
        def branch(field):
            return moved(field, "energy", -by), moved(field, "energy", by)

        return branch

    amount = shift[0]
    higher, beneath = lax.switch(amount - 1, [exchange(k + 1) for k in range(SMAX)], summed)
    along = jax.vmap(functools.partial(onward, upward=True))
    back = jax.vmap(functools.partial(onward, upward=False))
    higher = jnp.where(here + amount >= n_energy, along(higher), higher) * (1.0 / n_mom)
    beneath = jnp.where(here - amount < 0, back(beneath), beneath) * (1.0 / n_mom)
    emission = phonon_weight[0]
    absorption = phonon_weight[1]
    share = jnp.stack(
        [
            emission * higher[0] + absorption * beneath[0],
            emission * beneath[1] + absorption * higher[1],
        ]
    )
    from_before = moved(share, "mom", 1)
    from_after = moved(share, "mom", -1)
    far_less = moved(from_before[0], "mom", 1)
    far_great = moved(from_after[1], "mom", -1)
    sigma = jnp.stack([share, from_after, jnp.stack([far_less, far_great]), from_before])

    grid = (jnp.arange(count) * n_energy + here).astype(F32)
    energy = (grid + 0.5) * (2.0 * band_edge / total) - band_edge
    scalars = jnp.stack(
        [
            energy,
            jax.nn.sigmoid((left_level - energy) / thermal),
            jax.nn.sigmoid((right_level - energy) / thermal),
        ]
    )
    place = jnp.reshape(me, (1,)).astype(jnp.int32)
    less_new, great_new, flow = transport(place, scalars, sigma, hamiltonian[0], coupling[0])
    current = lax.psum(flow[0, 0] * (2.0 * band_edge / total), ("energy", "mom"))
    return (less_new[:, None, None], great_new[:, None, None], current)


def solution(mesh):
    return jax.shard_map(
        shards,
        mesh=mesh,
        in_specs=(
            P(None, "energy", "mom", None, None, None, None),
            P(None, "energy", "mom", None, None, None, None),
            P("mom", None, None, None, None),
            P("mom", None, None, None),
            P(),
            P(),
        ),
        out_specs=(
            P(None, "energy", "mom", None, None, None, None),
            P(None, "energy", "mom", None, None, None, None),
            P(),
        ),
        check_vma=False,
    )
```

time: 1430 us -> 189 us (0.13)
  other arithmetic: 905 us -> 7.7 us
  matrix products: 189 us -> 0 us
  waiting for transfers between devices: 171 us -> 41.1 us
  local copies, waits for them, and re-layouts: 83.7 us -> 7.1 us
  Pallas kernels: 0 us -> 39 us
  blocking collectives: 33 us -> 71.3 us
  between operations: 18.7 us -> 2.14 us
    another operation x61 -> x9, other arithmetic: 884 us -> 2.27 us  [the longest x2 1.81 us: shards(): jnp.stack([block(less, before), block(great, before) + first_b])]
    dot_general x188 -> x0, matrix products: 158 us -> none  [product(): return jnp.einsum('...ij,...jk->...ik', left, right, precision=precise)]
    all_gather x1 -> x0, waiting for transfers between devices: 64.6 us -> none  [shards(): lax.all_gather(jnp.stack([share_less, share_great], 0), 'mom', axis=2, ti...]
    all_to_all x1 -> x0, waiting for transfers between devices: 48.3 us -> none  [summed_on_arrival(): blocks = lax.all_to_all(in_blocks(array, dim, size), axis, 0, 0, tiled=True)]
    pallas_call x0 -> x1, Pallas kernels: none -> 39 us  [transport(): pl.pallas_call(kernel, out_shape=(blocks, blocks, jax.ShapeDtypeStruct((8...]
    psum x4 -> x1, blocking collectives: 33 us -> 71.3 us  [shards(): lax.psum(flow[0, 0] * (2.0 * band_edge / total), ('energy', 'mom'))]
    another operation x44 -> x0, local copies, waits for them, and re-layouts: 32.9 us -> none  [the longest x29 22.9 us: invert(): jax.scipy.linalg.solve_triangular(lower, middle, lower=True, trans=1)]
    another operation x32 -> x0, matrix products: 31.2 us -> none  [the longest x8 13.4 us: invert(): lower = jnp.linalg.cholesky(normal)]
  transfers between devices with their start and end apart: 8 -> 10, of which waited for: 6 -> 7; matrix products, arithmetic and copies ran while one was open for 1% -> 2% of each run, Pallas kernels for 0% -> 0%
where the time goes in v1:
time: 189 us; the launch traced here: 186 us
  blocking collectives  71.3 us (38%)
  waiting for transfers between devices  41.1 us (22%)
  Pallas kernels  39 us (21%)
  starting transfers between devices  17.9 us (9%)
  other arithmetic  7.7 us (4%)
  local copies, waits for them, and re-layouts  7.1 us (4%)
  between operations  2.14 us (1%)
    psum x1, blocking collectives, shards(): lax.psum(flow[0, 0] * (2.0 * band_edge / total), ('energy', 'mom'))  71.3 us
    ppermute x10, waiting for transfers between devices, moved(): lax.ppermute(array, axis, [(i, (i + by) % size) for i in range(size)])  41.1 us
    pallas_call x1, Pallas kernels, transport(): pl.pallas_call(kernel, out_shape=(blocks, blocks, jax.ShapeDtypeStruct((8...  39 us
    ppermute x10, starting transfers between devices, moved(): lax.ppermute(array, axis, [(i, (i + by) % size) for i in range(size)])  17.9 us
  transfers between devices with their start and end apart: 10, of which 7 were waited for; matrix products, arithmetic and copies ran while one was open for 2% of the time, Pallas kernels for 0%

profile of v1, /device:TPU:1, one launch (start us, length us, event | category | flops | bytes accessed | tf_op | source)
XLA Modules:
  0.0 186.3 jit_solution(12599160450742446873)
XLA Ops:
  0.7 1.7 copy.15
  2.4 2.8 %fusion.1 = (f32[4,4,128,128]{3,2,1,0:T(8,128)S(1)}, f32[4,4,128,128]{3,2,1,0:T(8,128)}) fusion(f32[4,4,2,128,128]{4,3,1,0,2:T(8,128)S(1)} %bitcast.76, pred[128,128]{1,0:T(8,128)(4,1)S(1)} %fusion.6, f32[4,4,2,128,128]{4,3,2,1,0:T(8,128)} %bitcast.77), kind=kLoop, calls=%fused_computation.13 | loop fusion | flops 524288 | bytes 6307840 | tf_op jit(solution)/shard_map/jit(_where)/select_n | solution.py:311
  5.2 1.2 dynamic-slice_bitcast_fusion
  6.4 4.6 %collective-permute-start.16 = (f32[4,128,128]{2,1,0:T(8,128)S(1)}, f32[4,128,128]{2,1,0:T(8,128)S(1)}, u32[]{:S(2)}, u32[]{:S(2)}) collective-permute-start(f32[4,128,128]{2,1,0:T(8,128)S(1)} %get-tuple-element.105), channel_id=1, source_target_pairs={{0,3},{1,0},{2,1},{3,2},{4,7},{5,4},{6,5},{7,6},{8,11},{9,8},{10,9... | collective-permute-start | bytes 786440 | tf_op jit(solution)/shard_map/ppermute | solution.py:286
  11.0 0.1 dynamic-slice_bitcast_fusion.1
  11.1 0.0 copy-start.2
  11.1 0.1 collective-permute-start.14
  11.2 4.8 %collective-permute-done.16 = f32[4,128,128]{2,1,0:T(8,128)S(1)} collective-permute-done((f32[4,128,128]{2,1,0:T(8,128)S(1)}, f32[4,128,128]{2,1,0:T(8,128)S(1)}, u32[]{:S(2)}, u32[]{:S(2)}) %collective-permute-start.16) | collective-permute-done | bytes 262176 | tf_op jit(solution)/shard_map/ppermute | solution.py:286
  16.0 1.0 fusion.4
  17.0 0.8 pad_maximum_fusion.2
  17.9 3.4 %collective-permute-start.17 = (f32[2,4,128,128]{3,2,1,0:T(8,128)}, f32[2,4,128,128]{3,2,1,0:T(8,128)S(1)}, u32[]{:S(2)}, u32[]{:S(2)}) collective-permute-start(f32[2,4,128,128]{3,2,1,0:T(8,128)} %pad_maximum_fusion.2), channel_id=1, source_target_pairs={{0,3},{1,0},{2,1},{3,2},{4,7},{5,4},{6,5},{7,6},{8,11},{9,8},{10,9... | collective-permute-start | bytes 1572872 | tf_op jit(solution)/shard_map/ppermute | solution.py:286
  21.3 0.0 collective-permute-done.14
  21.3 0.1 collective-permute-start.15
  22.1 0.0 copy-done.2
  22.1 0.6 fusion.8
  22.8 8.5 %collective-permute-done.17 = f32[2,4,128,128]{3,2,1,0:T(8,128)S(1)} collective-permute-done((f32[2,4,128,128]{3,2,1,0:T(8,128)}, f32[2,4,128,128]{3,2,1,0:T(8,128)S(1)}, u32[]{:S(2)}, u32[]{:S(2)}) %collective-permute-start.17) | collective-permute-done | bytes 524320 | tf_op jit(solution)/shard_map/ppermute | solution.py:286
  31.3 3.0 %collective-permute-done.15 = f32[2,4,128,128]{3,2,1,0:T(8,128)S(1)} collective-permute-done((f32[2,4,128,128]{3,2,1,0:T(8,128)S(1)}, f32[2,4,128,128]{3,2,1,0:T(8,128)S(1)}, u32[]{:S(2)}, u32[]{:S(2)}) %collective-permute-start.15) | collective-permute-done | bytes 524320 | tf_op jit(solution)/shard_map/ppermute | solution.py:286
  34.3 17.8 %conditional.1 = (f32[2,4,128,128]{3,2,1,0:T(8,128)}, f32[2,4,128,128]{3,2,1,0:T(8,128)}, f32[2,4,128,128]{3,2,1,0:T(8,128)S(1)}, f32[2,4,128,128]{3,2,1,0:T(8,128)S(1)}) conditional(s32[]{:T(128)} %clamp.3, (f32[2,4,128,128]{3,2,1,0:T(8,128)S(1)}, f32[2,4,128,128]{3,2,1,0:T(8,128)S(1)}, ...), branch_computations={%region_0.1_spmd, %region_1.2_spmd, %region_2.3_spmd, %region_3.4_... | conditional | flops 262144 | bytes 9699448 | solution.py:329
  34.3 0.1 add_add_fusion.6
  34.4 3.9 %collective-permute-start.13 = (f32[2,4,128,128]{3,2,1,0:T(8,128)S(1)}, f32[2,4,128,128]{3,2,1,0:T(8,128)}, u32[]{:S(2)}, u32[]{:S(2)}) collective-permute-start(f32[2,4,128,128]{3,2,1,0:T(8,128)S(1)} %add_add_fusion.6), channel_id=1, source_target_pairs={{0,28},{4,32},{8,36},{12,40},{16,44},{20,48},{24,52},{28,56},{32,6... | collective-permute-start | bytes 1572872 | tf_op jit(solution)/shard_map/cond/branch_6_fun/ppermute | solution.py:286
  38.3 2.4 %collective-permute-start.12 = (f32[2,4,128,128]{3,2,1,0:T(8,128)S(1)}, f32[2,4,128,128]{3,2,1,0:T(8,128)}, u32[]{:S(2)}, u32[]{:S(2)}) collective-permute-start(f32[2,4,128,128]{3,2,1,0:T(8,128)S(1)} %add_add_fusion.6), channel_id=1, source_target_pairs={{0,100},{4,104},{8,108},{12,112},{16,116},{20,120},{24,124},{28,0}... | collective-permute-start | bytes 1572872 | tf_op jit(solution)/shard_map/cond/branch_6_fun/ppermute | solution.py:286
  40.7 9.2 %collective-permute-done.13 = f32[2,4,128,128]{3,2,1,0:T(8,128)} collective-permute-done((f32[2,4,128,128]{3,2,1,0:T(8,128)S(1)}, f32[2,4,128,128]{3,2,1,0:T(8,128)}, u32[]{:S(2)}, u32[]{:S(2)}) %collective-permute-start.13) | collective-permute-done | bytes 524320 | tf_op jit(solution)/shard_map/cond/branch_6_fun/ppermute | solution.py:286
  50.0 1.0 slice.109
  51.0 0.0 collective-permute-done.12
  51.1 1.0 slice.108
  52.1 1.2 select_multiply_fusion
  53.3 1.3 fusion.3
  54.6 0.1 fusion.7
  54.7 0.1 collective-permute-start.18
  54.9 1.4 collective-permute-start.19
  56.3 9.3 %collective-permute-done.18 = f32[2,4,128,128]{3,2,1,0:T(8,128)S(1)} collective-permute-done((f32[2,4,128,128]{3,2,1,0:T(8,128)S(1)}, f32[2,4,128,128]{3,2,1,0:T(8,128)S(1)}, u32[]{:S(2)}, u32[]{:S(2)}) %collective-permute-start.18) | collective-permute-done | bytes 524320 | tf_op jit(solution)/shard_map/ppermute | solution.py:286
  65.6 1.3 collective-permute-start.21
  67.0 0.0 collective-permute-done.19
  67.0 0.4 collective-permute-start.20
  67.5 3.8 %collective-permute-done.21 = f32[4,128,128]{2,1,0:T(8,128)S(1)} collective-permute-done((f32[4,128,128]{2,1,0:T(8,128)S(1)}, f32[4,128,128]{2,1,0:T(8,128)S(1)}, u32[]{:S(2)}, u32[]{:S(2)}) %collective-permute-start.21) | collective-permute-done | bytes 262176 | tf_op jit(solution)/shard_map/ppermute | solution.py:286
  71.3 2.4 %collective-permute-done.20 = f32[4,128,128]{2,1,0:T(8,128)S(1)} collective-permute-done((f32[4,128,128]{2,1,0:T(8,128)S(1)}, f32[4,128,128]{2,1,0:T(8,128)S(1)}, u32[]{:S(2)}, u32[]{:S(2)}) %collective-permute-start.20) | collective-permute-done | bytes 262176 | tf_op jit(solution)/shard_map/ppermute | solution.py:286
  73.7 0.0 copy-start
  73.7 0.0 copy-start.1
  73.8 0.2 pad_maximum_fusion.sig_ref
  74.0 0.8 copy-done
  74.8 0.0 copy-done.1
  74.8 39.0 %shard_map.85 = (f32[4,4,2,128,128]{4,3,2,1,0:T(8,128)}, f32[4,4,2,128,128]{4,3,2,1,0:T(8,128)}, f32[8,128]{1,0:T(8,128)S(1)}) custom-call(s32[1]{0:T(128)} %bitcast.where_ref, f32[3,4]{1,0:T(4,128)S(1)} %pad_maximum_fusion.5.scal_ref, f32[4,2,4,128,128]{4,3,2,1,0:T(8,128)S(1)} %pad_maximum_fusion.sig_ref, f32[4,2,128,128]{3,2,1,0:T(8,128)S(1)} %bitcast.74, ...), custom_call_target="tpu_custom_call" | custom-call | flops 20000000000 | bytes 8000000 | tf_op jit(solution)/shard_map/pallas_call | solution.py:258
  113.8 0.5 slice.95
  115.0 71.3 %psum.7 = f32[]{:T(128)} all-reduce(f32[]{:T(128)} %bitcast.34), channel_id=1, replica_groups=mesh['energy'=32,'mom'=4] {'energy','mom'}, use_global_device_ids=true, to_apply=%region_7.8 | all-reduce | flops 1 | bytes 8 | tf_op jit(solution)/shard_map/psum | solution.py:359
  (12 shorter events, 0.3 us)
Async XLA Ops:
  6.4 9.6 %collective-permute-start.16 = (f32[4,128,128]{2,1,0:T(8,128)S(1)}, f32[4,128,128]{2,1,0:T(8,128)S(1)}, u32[]{:S(2)}, u32[]{:S(2)}) collective-permute-start(f32[4,128,128]{2,1,0:T(8,128)S(1)} %get-tuple-element.105), channel_id=1, source_target_pairs={{0,3},{1,0},{2,1},{3,2},{4,7},{5,4},{6,5},{7,6},{8,11},{9,8},{10,9... | collective-permute-start | bytes 786440 | tf_op jit(solution)/shard_map/ppermute | solution.py:286
  11.1 11.0 %copy-start.2 = (f32[2]{0:T(128)S(1)}, f32[2]{0:T(128)}, u32[]{:S(2)}) copy-start(f32[2]{0:T(128)} %param.18) | copy-start | bytes 28
  11.1 10.1 %collective-permute-start.14 = (f32[4,128,128]{2,1,0:T(8,128)S(1)}, f32[4,128,128]{2,1,0:T(8,128)S(1)}, u32[]{:S(2)}, u32[]{:S(2)}) collective-permute-start(f32[4,128,128]{2,1,0:T(8,128)S(1)} %get-tuple-element.103), channel_id=1, source_target_pairs={{0,1},{1,2},{2,3},{3,0},{4,5},{5,6},{6,7},{7,4},{8,9},{9,10},{10,1... | collective-permute-start | bytes 786440 | tf_op jit(solution)/shard_map/ppermute | solution.py:286
  17.9 13.5 %collective-permute-start.17 = (f32[2,4,128,128]{3,2,1,0:T(8,128)}, f32[2,4,128,128]{3,2,1,0:T(8,128)S(1)}, u32[]{:S(2)}, u32[]{:S(2)}) collective-permute-start(f32[2,4,128,128]{3,2,1,0:T(8,128)} %pad_maximum_fusion.2), channel_id=1, source_target_pairs={{0,3},{1,0},{2,1},{3,2},{4,7},{5,4},{6,5},{7,6},{8,11},{9,8},{10,9... | collective-permute-start | bytes 1572872 | tf_op jit(solution)/shard_map/ppermute | solution.py:286
  21.3 13.0 %collective-permute-start.15 = (f32[2,4,128,128]{3,2,1,0:T(8,128)S(1)}, f32[2,4,128,128]{3,2,1,0:T(8,128)S(1)}, u32[]{:S(2)}, u32[]{:S(2)}) collective-permute-start(f32[2,4,128,128]{3,2,1,0:T(8,128)S(1)} %pad_maximum_fusion.1), channel_id=1, source_target_pairs={{0,1},{1,2},{2,3},{3,0},{4,5},{5,6},{6,7},{7,4},{8,9},{9,10},{10,1... | collective-permute-start | bytes 1572872 | tf_op jit(solution)/shard_map/ppermute | solution.py:286
  34.4 15.6 %collective-permute-start.13 = (f32[2,4,128,128]{3,2,1,0:T(8,128)S(1)}, f32[2,4,128,128]{3,2,1,0:T(8,128)}, u32[]{:S(2)}, u32[]{:S(2)}) collective-permute-start(f32[2,4,128,128]{3,2,1,0:T(8,128)S(1)} %add_add_fusion.6), channel_id=1, source_target_pairs={{0,28},{4,32},{8,36},{12,40},{16,44},{20,48},{24,52},{28,56},{32,6... | collective-permute-start | bytes 1572872 | tf_op jit(solution)/shard_map/cond/branch_6_fun/ppermute | solution.py:286
  38.3 12.7 %collective-permute-start.12 = (f32[2,4,128,128]{3,2,1,0:T(8,128)S(1)}, f32[2,4,128,128]{3,2,1,0:T(8,128)}, u32[]{:S(2)}, u32[]{:S(2)}) collective-permute-start(f32[2,4,128,128]{3,2,1,0:T(8,128)S(1)} %add_add_fusion.6), channel_id=1, source_target_pairs={{0,100},{4,104},{8,108},{12,112},{16,116},{20,120},{24,124},{28,0}... | collective-permute-start | bytes 1572872 | tf_op jit(solution)/shard_map/cond/branch_6_fun/ppermute | solution.py:286
  54.7 10.9 %collective-permute-start.18 = (f32[2,4,128,128]{3,2,1,0:T(8,128)S(1)}, f32[2,4,128,128]{3,2,1,0:T(8,128)S(1)}, u32[]{:S(2)}, u32[]{:S(2)}) collective-permute-start(f32[2,4,128,128]{3,2,1,0:T(8,128)S(1)} %get-tuple-element.108), channel_id=1, source_target_pairs={{0,3},{1,0},{2,1},{3,2},{4,7},{5,4},{6,5},{7,6},{8,11},{9,8},{10,9... | collective-permute-start | bytes 1572872 | tf_op jit(solution)/shard_map/ppermute | solution.py:286
  54.9 12.1 %collective-permute-start.19 = (f32[2,4,128,128]{3,2,1,0:T(8,128)S(1)}, f32[2,4,128,128]{3,2,1,0:T(8,128)S(1)}, u32[]{:S(2)}, u32[]{:S(2)}) collective-permute-start(f32[2,4,128,128]{3,2,1,0:T(8,128)S(1)} %get-tuple-element.108), channel_id=1, source_target_pairs={{0,1},{1,2},{2,3},{3,0},{4,5},{5,6},{6,7},{7,4},{8,9},{9,10},{10,1... | collective-permute-start | bytes 1572872 | tf_op jit(solution)/shard_map/ppermute | solution.py:286
  65.6 5.6 %collective-permute-start.21 = (f32[4,128,128]{2,1,0:T(8,128)S(1)}, f32[4,128,128]{2,1,0:T(8,128)S(1)}, u32[]{:S(2)}, u32[]{:S(2)}) collective-permute-start(f32[4,128,128]{2,1,0:T(8,128)S(1)} %slice_bitcast_fusion.4), channel_id=1, source_target_pairs={{0,3},{1,0},{2,1},{3,2},{4,7},{5,4},{6,5},{7,6},{8,11},{9,8},{10,9... | collective-permute-start | bytes 786440 | tf_op jit(solution)/shard_map/ppermute | solution.py:286
  67.0 6.7 %collective-permute-start.20 = (f32[4,128,128]{2,1,0:T(8,128)S(1)}, f32[4,128,128]{2,1,0:T(8,128)S(1)}, u32[]{:S(2)}, u32[]{:S(2)}) collective-permute-start(f32[4,128,128]{2,1,0:T(8,128)S(1)} %slice_bitcast_fusion.5), channel_id=1, source_target_pairs={{0,1},{1,2},{2,3},{3,0},{4,5},{5,6},{6,7},{7,4},{8,9},{9,10},{10,1... | collective-permute-start | bytes 786440 | tf_op jit(solution)/shard_map/ppermute | solution.py:286
  73.7 1.0 copy-start
  73.7 1.1 copy-start.1

commit v2 on v1

--- a/solution.py
+++ b/solution.py
@@ -59,7 +59,7 @@
 
 
 def kernel(
-    where_ref, scal_ref, sig_ref, ham_ref, hop_ref,
+    scal_ref, sig_ref, ham_ref, hop_ref,
     less_ref, great_ref, flow_ref,
     hop_f, sys_f, inv_f, tmp_f, inj_f, gr_f, t_f, l_f, full_f,
     inv, gl, gr, folded_r, folded_l,
@@ -70,7 +70,6 @@
     rows = lax.broadcasted_iota(jnp.int32, (W, W), 0)
     cols = lax.broadcasted_iota(jnp.int32, (W, W), 1)
     eye = jnp.where(rows == cols, 1.0, 0.0).astype(F32)
-    here = where_ref[0]
 
     def unpack(value):
         turned = value.T
@@ -81,12 +80,11 @@
     store(hop_f, hop_ref[0].T, -hop_ref[1].T)
 
     def forward(slab, last):
-        place = lax.rem(slab - here + slabs, slabs)
         at_left = jnp.where(slab == 0, 1.0, 0.0)
         norms = []
         for e in energies:
-            less = unpack(sig_ref[place, 0, e])
-            great = unpack(sig_ref[place, 1, e])
+            less = unpack(sig_ref[slab, 0, e])
+            great = unpack(sig_ref[slab, 1, e])
             fill = scal_ref[2, e] if last else at_left * scal_ref[1, e]
             contact = contact_rate if last else at_left * contact_rate
             sys_r = scal_ref[0, e] * eye - ham_ref[slab, 0] - 0.5 * (great[0] - less[0])
@@ -249,7 +247,7 @@
     lax.fori_loop(1, slabs, up, 0)
 
 
-def transport(place, scalars, sigma, hamiltonian, coupling):
+def transport(scalars, sigma, hamiltonian, coupling):
     slabs, _, count = sigma.shape[:3]
     form = (2 * W, 2 * W)
     vmem = pl.BlockSpec(memory_space=pltpu.VMEM)
@@ -258,7 +256,7 @@
     return pl.pallas_call(
         kernel,
         out_shape=(blocks, blocks, jax.ShapeDtypeStruct((8, W), F32)),
-        in_specs=[smem, smem, vmem, vmem, vmem],
+        in_specs=[smem, vmem, vmem, vmem],
         out_specs=(vmem, vmem, vmem),
         scratch_shapes=[
             pltpu.VMEM(form, BF),
@@ -278,73 +276,217 @@
         ],
         compiler_params=pltpu.CompilerParams(vmem_limit_bytes=48 * 1024 * 1024),
         cost_estimate=pl.CostEstimate(flops=20_000_000_000, bytes_accessed=8_000_000, transcendentals=0),
-    )(place, scalars, sigma, hamiltonian, coupling)
-
-
-def moved(array, axis, by):
-    size = lax.axis_size(axis)
-    return lax.ppermute(array, axis, [(i, (i + by) % size) for i in range(size)])
-
-
-def block(array, index):
-    return lax.dynamic_index_in_dim(array, index, 0, keepdims=False)
-
-
-def onward(field, upward):
-    blank = jnp.zeros_like(field[:1])
-    if upward:
-        return jnp.concatenate([field[1:], blank], 0)
-    return jnp.concatenate([blank, field[:-1]], 0)
+    )(scalars, sigma, hamiltonian, coupling)
+
+
+MESH = pl.DeviceIdType.MESH
+CHUNKS = 4
+
+
+def exchange_kernel(
+    by, n_energy, n_mom,
+    weight_ref, less_ref, great_ref, sigma_ref,
+    pack, near_a, near_b, half_a, half_b, share, high, low, send_sem, recv_sem,
+):
+    place = lax.axis_index("energy")
+    me = lax.axis_index("mom")
+    count = less_ref.shape[0]
+    depth = W // CHUNKS
+    after = lax.rem(me + 1, n_mom)
+    before = lax.rem(me + n_mom - 1, n_mom)
+    across = lax.rem(me + 2, n_mom)
+    over = {"energy": lax.rem(place + by, n_energy)}
+    under = {"energy": lax.rem(place - by + n_energy, n_energy)}
+    wrapped_up = lax.div(place + by, n_energy)
+    wrapped_down = 1 - lax.div(place - by + n_energy, n_energy)
+    kept_up = (1 - wrapped_up).astype(F32)
+    kept_down = (1 - wrapped_down).astype(F32)
+    emission = weight_ref[0] * (1.0 / n_mom)
+    absorption = weight_ref[1] * (1.0 / n_mom)
+
+    barrier = pltpu.get_barrier_semaphore()
+    for peer in ({"mom": after}, {"mom": before}, over, under):
+        pl.semaphore_signal(barrier, inc=1, device_id=peer, device_id_type=MESH)
+
+    def send(kind, chunk, source, target, peer):
+        copy = pltpu.make_async_remote_copy(
+            src_ref=source,
+            dst_ref=target,
+            send_sem=send_sem.at[kind, chunk],
+            recv_sem=recv_sem.at[kind, chunk],
+            device_id=peer,
+            device_id_type=MESH,
+        )
+        copy.start()
+        return copy
+
+    sent = {}
+    rows = lax.broadcasted_iota(jnp.int32, (depth, W), 0)
+    cols = lax.broadcasted_iota(jnp.int32, (depth, W), 1)
+    for c in range(CHUNKS):
+        span = slice(c * depth, (c + 1) * depth)
+        upper = cols > rows + c * depth
+        for slab in range(n_mom):
+            for kind, ref in enumerate((less_ref, great_ref)):
+                pack[c, slab, kind] = jnp.where(upper, ref[:, slab, 0, span], ref[:, slab, 1, span])
+        if c == 0:
+            pl.semaphore_wait(barrier, 4)
+        sent[0, c] = send(0, c, pack.at[c, across, 0], near_a.at[c], {"mom": after})
+        sent[1, c] = send(1, c, pack.at[c, across, 1], near_b.at[c], {"mom": before})
+    for c in range(CHUNKS):
+        sent[0, c].wait_recv()
+        pack[c, after, 0] = pack[c, after, 0] + near_a[c]
+        sent[1, c].wait_recv()
+        pack[c, before, 1] = pack[c, before, 1] + near_b[c]
+        sent[2, c] = send(2, c, pack.at[c, after], half_a.at[c], {"mom": after})
+        sent[3, c] = send(3, c, pack.at[c, before], half_b.at[c], {"mom": before})
+    for c in range(CHUNKS):
+        sent[2, c].wait_recv()
+        sent[3, c].wait_recv()
+        share[c] = pack[c, me] + (half_a[c] + half_b[c])
+        sent[4, c] = send(4, c, share.at[c], high.at[c], under)
+        sent[5, c] = send(5, c, share.at[c], low.at[c], over)
+    for c in range(CHUNKS):
+        span = slice(c * depth, (c + 1) * depth)
+        sent[4, c].wait_recv()
+        sent[5, c].wait_recv()
+        for j in range(count):
+            if j < count - 1:
+                up = [high[c, kind, j + wrapped_up] for kind in range(2)]
+            else:
+                up = [high[c, kind, j] * kept_up for kind in range(2)]
+            if j > 0:
+                down = [low[c, kind, j - wrapped_down] for kind in range(2)]
+            else:
+                down = [low[c, kind, j] * kept_down for kind in range(2)]
+            sigma_ref[me, 0, j, span] = emission * up[0] + absorption * down[0]
+            sigma_ref[me, 1, j, span] = emission * down[1] + absorption * up[1]
+        mine = sigma_ref.at[me, :, :, span]
+        sent[6, c] = send(6, c, mine, mine, {"mom": after})
+        sent[7, c] = send(7, c, mine, mine, {"mom": before})
+    for c in range(CHUNKS):
+        span = slice(c * depth, (c + 1) * depth)
+        sent[6, c].wait_recv()
+        part = sigma_ref.at[before, 0, :, span]
+        sent[8, c] = send(8, c, part, part, {"mom": after})
+        sent[7, c].wait_recv()
+        part = sigma_ref.at[after, 1, :, span]
+        sent[9, c] = send(9, c, part, part, {"mom": before})
+    for c in range(CHUNKS):
+        sent[8, c].wait_recv()
+        sent[9, c].wait_recv()
+    for copy in sent.values():
+        copy.wait_send()
+
+
+def exchange(by, n_energy, n_mom, weight, lesser, greater):
+    count = lesser.shape[0]
+    depth = W // CHUNKS
+    vmem = pl.BlockSpec(memory_space=pltpu.VMEM)
+    half = (CHUNKS, count, depth, W)
+    whole = (CHUNKS, 2, count, depth, W)
+    return pl.pallas_call(
+        functools.partial(exchange_kernel, by, n_energy, n_mom),
+        out_shape=jax.ShapeDtypeStruct((n_mom, 2, count, W, W), F32),
+        in_specs=[pl.BlockSpec(memory_space=pltpu.SMEM), vmem, vmem],
+        out_specs=vmem,
+        scratch_shapes=[
+            pltpu.VMEM((CHUNKS, n_mom, 2, count, depth, W), F32),
+            pltpu.VMEM(half, F32),
+            pltpu.VMEM(half, F32),
+            pltpu.VMEM(whole, F32),
+            pltpu.VMEM(whole, F32),
+            pltpu.VMEM(whole, F32),
+            pltpu.VMEM(whole, F32),
+            pltpu.VMEM(whole, F32),
+            pltpu.SemaphoreType.DMA((10, CHUNKS)),
+            pltpu.SemaphoreType.DMA((10, CHUNKS)),
+        ],
+        compiler_params=pltpu.CompilerParams(
+            collective_id=by, has_side_effects=True, vmem_limit_bytes=32 * 1024 * 1024
+        ),
+    )(weight, lesser, greater)
+
+
+def total_kernel(n_mom, flow_ref, total_ref, first, second, partial, send_sem, recv_sem):
+    place = lax.axis_index("energy")
+    me = lax.axis_index("mom")
+    inner = second.shape[0]
+    outer = first.shape[0]
+    low = lax.rem(place, inner)
+    high = lax.div(place, inner)
+    slot = high * n_mom + me
+
+    def outer_peer(step):
+        other = lax.rem(slot + step, outer)
+        return other, {"energy": lax.div(other, n_mom) * inner + low, "mom": lax.rem(other, n_mom)}
+
+    def inner_peer(step):
+        other = lax.rem(low + step, inner)
+        return other, {"energy": high * inner + other, "mom": me}
+
+    barrier = pltpu.get_barrier_semaphore()
+    for step in range(1, outer):
+        pl.semaphore_signal(barrier, inc=1, device_id=outer_peer(step)[1], device_id_type=MESH)
+    for step in range(1, inner):
+        pl.semaphore_signal(barrier, inc=1, device_id=inner_peer(step)[1], device_id_type=MESH)
+    pl.semaphore_wait(barrier, outer + inner - 2)
+
+    def round_of(source, slots, size, own, peer, base):
+        def copy(index, step):
+            return pltpu.make_async_remote_copy(
+                src_ref=source,
+                dst_ref=slots.at[index],
+                send_sem=send_sem.at[base + step],
+                recv_sem=recv_sem.at[base + index],
+                device_id=peer(step)[1],
+                device_id_type=MESH,
+            )
+
+        for step in range(1, size):
+            copy(own, step).start()
+        slots[own] = source[...]
+        for step in range(1, size):
+            copy(peer(step)[0], step).wait_recv()
+        result = slots[0]
+        for index in range(1, size):
+            result = result + slots[index]
+        for step in range(1, size):
+            copy(own, step).wait_send()
+        return result
+
+    partial[...] = round_of(flow_ref, first, outer, slot, outer_peer, 0)
+    total_ref[...] = round_of(partial, second, inner, low, inner_peer, outer)
+
+
+def summed(flow, n_energy, n_mom):
+    inner = 8
+    outer = n_energy // inner * n_mom
+    vmem = pl.BlockSpec(memory_space=pltpu.VMEM)
+    return pl.pallas_call(
+        functools.partial(total_kernel, n_mom),
+        out_shape=jax.ShapeDtypeStruct(flow.shape, F32),
+        in_specs=[vmem],
+        out_specs=vmem,
+        scratch_shapes=[
+            pltpu.VMEM((outer,) + flow.shape, F32),
+            pltpu.VMEM((inner,) + flow.shape, F32),
+            pltpu.VMEM(flow.shape, F32),
+            pltpu.SemaphoreType.DMA((outer + inner,)),
+            pltpu.SemaphoreType.DMA((outer + inner,)),
+        ],
+        compiler_params=pltpu.CompilerParams(collective_id=SMAX + 1, has_side_effects=True),
+    )(flow)
 
 
 def shards(lesser, greater, hamiltonian, coupling, shift, phonon_weight):
     n_energy = lax.axis_size("energy")
     n_mom = lax.axis_size("mom")
     here = lax.axis_index("energy")
-    me = lax.axis_index("mom")
     count = lesser.shape[0]
     total = count * n_energy
-    upper = jnp.triu(jnp.ones((W, W), jnp.bool_), 1)
-
-    def packed(field):
-        field = field[:, 0, 0]
-        return jnp.swapaxes(jnp.where(upper, field[:, :, 0], field[:, :, 1]), 0, 1)
-
-    less = packed(lesser)
-    great = packed(greater)
-    after, before, across = (me + 1) % n_mom, (me + n_mom - 1) % n_mom, (me + 2) % n_mom
-    first_a = moved(block(less, across), "mom", 1)
-    first_b = moved(block(great, across), "mom", -1)
-    second_a = moved(jnp.stack([block(less, after) + first_a, block(great, after)]), "mom", 1)
-    second_b = moved(jnp.stack([block(less, before), block(great, before) + first_b]), "mom", -1)
-    summed = jnp.stack([block(less, me), block(great, me)]) + (second_a + second_b)
-
-    def exchange(by):
-        def branch(field):
-            return moved(field, "energy", -by), moved(field, "energy", by)
-
-        return branch
-
-    amount = shift[0]
-    higher, beneath = lax.switch(amount - 1, [exchange(k + 1) for k in range(SMAX)], summed)
-    along = jax.vmap(functools.partial(onward, upward=True))
-    back = jax.vmap(functools.partial(onward, upward=False))
-    higher = jnp.where(here + amount >= n_energy, along(higher), higher) * (1.0 / n_mom)
-    beneath = jnp.where(here - amount < 0, back(beneath), beneath) * (1.0 / n_mom)
-    emission = phonon_weight[0]
-    absorption = phonon_weight[1]
-    share = jnp.stack(
-        [
-            emission * higher[0] + absorption * beneath[0],
-            emission * beneath[1] + absorption * higher[1],
-        ]
-    )
-    from_before = moved(share, "mom", 1)
-    from_after = moved(share, "mom", -1)
-    far_less = moved(from_before[0], "mom", 1)
-    far_great = moved(from_after[1], "mom", -1)
-    sigma = jnp.stack([share, from_after, jnp.stack([far_less, far_great]), from_before])
-
+    branches = [functools.partial(exchange, k + 1, n_energy, n_mom) for k in range(SMAX)]
+    sigma = lax.switch(shift[0] - 1, branches, phonon_weight, lesser[:, 0, 0], greater[:, 0, 0])
     grid = (jnp.arange(count) * n_energy + here).astype(F32)
     energy = (grid + 0.5) * (2.0 * band_edge / total) - band_edge
     scalars = jnp.stack(
@@ -354,9 +496,8 @@
             jax.nn.sigmoid((right_level - energy) / thermal),
         ]
     )
-    place = jnp.reshape(me, (1,)).astype(jnp.int32)
-    less_new, great_new, flow = transport(place, scalars, sigma, hamiltonian[0], coupling[0])
-    current = lax.psum(flow[0, 0] * (2.0 * band_edge / total), ("energy", "mom"))
+    less_new, great_new, flow = transport(scalars, sigma, hamiltonian[0], coupling[0])
+    current = summed(flow, n_energy, n_mom)[0, 0] * (2.0 * band_edge / total)
     return (less_new[:, None, None], great_new[:, None, None], current)
 
 

time: 189 us -> 107 us (0.57); the launches traced: 186 us -> 109 us
  blocking collectives: 71.3 us -> 0 us
  Pallas kernels: 39 us -> 104 us
  waiting for transfers between devices: 41.1 us -> 0 us
  starting transfers between devices: 17.9 us -> 0 us
  other arithmetic: 7.7 us -> 0.05 us
  local copies, waits for them, and re-layouts: 7.1 us -> 1.78 us
    psum x1 -> x0, blocking collectives: 71.3 us -> none  [shards(): lax.psum(flow[0, 0] * (2.0 * band_edge / total), ('energy', 'mom'))]
    pallas_call x0 -> x2, Pallas kernels: none -> 64.2 us  [the longest x1 52.8 us: exchange(): pl.pallas_call(functools.partial(exchange_kernel, by, n_energy, n_mom), o...]
    ppermute x10 -> x0, waiting for transfers between devices: 41.1 us -> none  [moved(): lax.ppermute(array, axis, [(i, (i + by) % size) for i in range(size)])]
    ppermute x10 -> x0, starting transfers between devices: 17.9 us -> none  [moved(): lax.ppermute(array, axis, [(i, (i + by) % size) for i in range(size)])]
    select_n x2 -> x0, other arithmetic: 2.82 us -> none  [the longest x1 2.8 us: packed(): return jnp.swapaxes(jnp.where(upper, field[:, :, 0], field[:, :, 1]), 0, 1)]
    another operation x8 -> x0, other arithmetic: 2.26 us -> none  [the longest x2 1.81 us: shards(): jnp.stack([block(less, before), block(great, before) + first_b])]
    slice x4 -> x1, local copies, waits for them, and re-layouts: 3.21 us -> 1.19 us  [shards(): current = summed(flow, n_energy, n_mom)[0, 0] * (2.0 * band_edge / total)]
    unnamed x7 -> x6, local copies, waits for them, and re-layouts: 2.57 us -> 0.6 us
  transfers between devices with their start and end apart: 10 -> 0, of which waited for: 7 -> 0; matrix products, arithmetic and copies ran while one was open for 2% -> 0% of each run, Pallas kernels for 0% -> 0%
where the time goes in v2:
time: 107 us; the launch traced here: 109 us
  Pallas kernels  104 us (97%)
  between operations  3.12 us (3%)
  local copies, waits for them, and re-layouts  1.78 us (2%)
    pallas_call x1, Pallas kernels, exchange(): pl.pallas_call(functools.partial(exchange_kernel, by, n_energy, n_mom), o...  52.8 us
    pallas_call x1, Pallas kernels, transport(): pl.pallas_call(kernel, out_shape=(blocks, blocks, jax.ShapeDtypeStruct((8...  39.4 us
    pallas_call x1, Pallas kernels, summed(): pl.pallas_call(functools.partial(total_kernel, n_mom), out_shape=jax.Shap...  11.4 us

profile of v2, /device:TPU:1, one launch (start us, length us, event | category | flops | bytes accessed | tf_op | source)
XLA Modules:
  0.0 108.6 jit_solution(6026692062941263476)
XLA Ops:
  1.3 0.0 copy-start.1
  1.4 0.0 copy-start.2
  1.4 52.9 %conditional.1 = (f32[4,2,4,128,128]{4,3,2,1,0:T(8,128)S(1)}) conditional(s32[]{:T(128)} %bitcast, (f32[2]{0:T(128)}, f32[4,4,2,128,128]{4,3,2,1,0:T(8,128)}, f32[4,4,2,128,128]{4,3,2,1,0:T(8,128)}) %tuple.47, (f32[2]{0:T(128)}, f32[4,4,2,128,128]{4,3,2,1,0:T(8,128)}, f32[4,4,2,128,128]{4,3,2,1,0:T(8,128)}) %tuple.48, ...), branch_computations={%region_0.0_spmd, %region_1.0_spmd, %region_2.0_spmd, %region_3.0_... | conditional | bytes 8 | solution.py:489
  1.4 52.8 %branch_4_fun.1 = f32[4,2,4,128,128]{4,3,2,1,0:T(8,128)S(1)} custom-call(f32[2]{0:T(128)} %get-tuple-element.62.weight_ref, f32[4,4,2,128,128]{4,3,2,1,0:T(8,128)} %get-tuple-element.63.less_ref, f32[4,4,2,128,128]{4,3,2,1,0:T(8,128)} %get-tuple-element.64.great_ref), custom_call_target="tpu_custom_call" | custom-call | tf_op jit(solution)/shard_map/cond/branch_4_fun/pallas_call | solution.py:388
  54.2 0.0 copy-done.1
  54.2 0.0 copy-done.2
  54.3 39.4 %shard_map.85 = (f32[4,4,2,128,128]{4,3,2,1,0:T(8,128)}, f32[4,4,2,128,128]{4,3,2,1,0:T(8,128)}, f32[8,128]{1,0:T(8,128)S(1)}) custom-call(f32[3,4]{1,0:T(4,128)S(1)} %pad_maximum_fusion.scal_ref, f32[4,2,4,128,128]{4,3,2,1,0:T(8,128)S(1)} %get-tuple-element.85.sig_ref, f32[4,2,128,128]{3,2,1,0:T(8,128)S(1)} %bitcast.12, f32[2,128,128]{2,1,0:T(8,128)S(1)} %bitcast.13), custom_call_target="tpu_custom_call" | custom-call | flops 20000000000 | bytes 8000000 | tf_op jit(solution)/shard_map/pallas_call | solution.py:256
  93.7 0.0 copy-start
  93.7 0.6 copy-done
  94.3 11.4 %shard_map.86 = f32[8,128]{1,0:T(8,128)} custom-call(f32[8,128]{1,0:T(8,128)} %copy-done), custom_call_target="tpu_custom_call" | custom-call | tf_op jit(solution)/shard_map/pallas_call | solution.py:466
  105.7 1.2 %slice.3 = f32[1,1]{1,0:T(1,128)} slice(f32[8,128]{1,0:T(8,128)} %shard_map.86), slice={[0:1], [0:1]} | slice | bytes 8 | tf_op jit(solution)/shard_map/slice | solution.py:500
  (3 shorter events, 0.0 us)
Async XLA Ops:
  1.3 52.9 %copy-start.1 = (f32[1,4,2,128,128]{4,3,2,1,0:T(8,128)S(1)}, f32[1,4,2,128,128]{4,3,2,1,0:T(8,128)}, u32[]{:S(2)}) copy-start(f32[1,4,2,128,128]{4,3,2,1,0:T(8,128)} %param.15) | copy-start | bytes 1572868
  1.4 52.9 %copy-start.2 = (f32[1,2,128,128]{3,2,1,0:T(8,128)S(1)}, f32[1,2,128,128]{3,2,1,0:T(8,128)}, u32[]{:S(2)}) copy-start(f32[1,2,128,128]{3,2,1,0:T(8,128)} %param.16) | copy-start | bytes 393220
  93.7 0.6 copy-start

commit v3 on v2

v3 whole, which is shorter than its diff:
```python
import functools

import jax
import jax.numpy as jnp
from jax import lax
from jax.experimental import pallas as pl
from jax.experimental.pallas import tpu as pltpu
from jax.sharding import PartitionSpec as P

SMAX = 7
broaden = 0.2
contact_rate = 0.5
left_level = 0.3
right_level = -0.3
thermal = 0.1
band_edge = 2.0

W = 128
BF = jnp.bfloat16
F32 = jnp.float32
LEAST = 0.03


def store(ref, real, imag):
    for row, part in ((0, real), (W, imag)):
        high = part.astype(BF)
        ref[row : row + W, :W] = high
        ref[row : row + W, W:] = (part - high.astype(F32)).astype(BF)


def store_high(ref, real, imag):
    ref[:W, :W] = real.astype(BF)
    ref[W:, :W] = imag.astype(BF)


def product(left, right, dagger=False, high=False):
    if high:
        lhs = left[:, :W]
    else:
        whole = left[...]
        lhs = jnp.concatenate([whole, whole], 1)
    if dagger:
        up = right[:, :W]
        low = None if high else right[:, W:]
        rhs = up if high else jnp.concatenate([up, up, low, low], 1)
        dims = (((1,), (1,)), ((), ()))
    else:
        up = jnp.concatenate([right[:W, :W], right[W:, :W]], 1)
        if high:
            rhs = up
        else:
            low = jnp.concatenate([right[:W, W:], right[W:, W:]], 1)
            rhs = jnp.concatenate([up, up, low, low], 0)
        dims = (((1,), (0,)), ((), ()))
    full = lax.dot_general(lhs, rhs, dims, preferred_element_type=F32)
    if dagger:
        return full[:W, :W] + full[W:, W:], full[W:, :W] - full[:W, W:]
    return full[:W, :W] - full[W:, W:], full[:W, W:] + full[W:, :W]


FAST_LOW = 0.006
FAST_TOP = 0.4
FAST_GROW = 5
FAST_REFINE = 2
RESIDUAL = 1.0e-4


def schedule():
    lowest, steps = FAST_LOW, []
    for step in range(FAST_GROW):
        used = max(lowest, LEAST)
        a = 4.0 / (1.0 + used)
        b = a / (1.0 + used)
        lowest = min(lowest * (a - b * lowest), b * used)
        centre = 2.0 / (1.0 + lowest) if step == FAST_GROW - 1 else 1.0
        steps.append((a * centre, b * centre))
    return steps


class Solver:
    names = (
        "hop_f", "sys_f", "inv_f", "tmp_f", "inj_f", "gr_f", "t_f", "l_f", "full_f",
        "inv", "gl", "gr", "folded_r", "folded_l", "rho",
    )

    def __init__(self, fast, sigma, scal, ham, less, great, scratch, base=0):
        self.fast = fast
        self.sigma = sigma
        self.scal = lambda row, e: scal[row, base + e]
        self.ham = ham
        self.less = less
        self.great = great
        for name, ref in zip(self.names, scratch, strict=True):
            setattr(self, name, ref)
        self.count = self.inv.shape[0]
        self.slabs = ham.shape[0]
        self.energies = range(self.count)
        self.rows = lax.broadcasted_iota(jnp.int32, (W, W), 0)
        self.cols = lax.broadcasted_iota(jnp.int32, (W, W), 1)
        self.eye = jnp.where(self.rows == self.cols, 1.0, 0.0).astype(F32)

    @classmethod
    def scratch(cls, count, slabs):
        form = (2 * W, 2 * W)
        blocks = (count, 2, W, W)
        few = pltpu.VMEM((count,) + form, BF)
        many = pltpu.VMEM((slabs, count) + form, BF)
        every = pltpu.VMEM((slabs,) + blocks, F32)
        own = pltpu.VMEM(blocks, F32)
        return [
            pltpu.VMEM(form, BF), few, few, few, few, many, many, many,
            pltpu.VMEM((2, count) + form, BF), own, every, every, own, own, pltpu.VMEM((8, W), F32),
        ]

    def start(self, hop):
        store(self.hop_f, hop[0].T, -hop[1].T)
        self.rho[...] = jnp.zeros((8, W), F32)

    def block(self, slab, kind, e):
        value = self.sigma(slab, kind, e)
        turned = value.T
        real = jnp.where(self.rows < self.cols, value, jnp.where(self.rows > self.cols, -turned, 0.0))
        imag = jnp.where(self.rows >= self.cols, value, turned)
        return real, imag

    def grow_step(self, a, b):
        for e in self.energies:
            real, imag = product(self.inv_f.at[e], self.sys_f.at[e], high=True)
            store_high(self.tmp_f.at[e], real, imag)
        for e in self.energies:
            real, imag = product(self.tmp_f.at[e], self.inv_f.at[e], high=True)
            real = a * self.inv[e, 0] - b * real
            imag = a * self.inv[e, 1] - b * imag
            self.inv[e, 0] = real
            self.inv[e, 1] = imag
            store_high(self.inv_f.at[e], real, imag)

    def whole_form(self):
        for e in self.energies:
            store(self.inv_f.at[e], self.inv[e, 0], self.inv[e, 1])

    def refine_step(self):
        sizes = []
        for e in self.energies:
            real, imag = product(self.inv_f.at[e], self.sys_f.at[e])
            real = self.eye - real
            sizes.append(jnp.sum(real * real + imag * imag, axis=0, keepdims=True))
            store_high(self.tmp_f.at[e], real, -imag)
        for e in self.energies:
            real, imag = product(self.tmp_f.at[e], self.inv_f.at[e], high=True)
            real = self.inv[e, 0] + real
            imag = self.inv[e, 1] + imag
            self.inv[e, 0] = real
            self.inv[e, 1] = imag
            store(self.inv_f.at[e], real, imag)
        return sizes

    def invert(self, midway):
        norms = []
        for e in self.energies:
            real, imag = product(self.inv_f.at[e], self.sys_f.at[e], high=True)
            norms.append(jnp.sum(jnp.sqrt(real * real + imag * imag), axis=0, keepdims=True))
            if self.fast:
                store_high(self.tmp_f.at[e], real, imag)
        bound = 1.05 * jnp.max(functools.reduce(jnp.maximum, norms))
        if self.fast:
            steps = schedule()
            scale = 1.0 / (FAST_TOP * bound)
            first = steps[0][0] * scale
            second = steps[0][1] * scale * scale
            for e in self.energies:
                real, imag = product(self.tmp_f.at[e], self.inv_f.at[e], high=True)
                real = first * self.inv[e, 0] - second * real
                imag = first * self.inv[e, 1] - second * imag
                self.inv[e, 0] = real
                self.inv[e, 1] = imag
                store_high(self.inv_f.at[e], real, imag)
            for place, (a, b) in enumerate(steps[1:]):
                self.grow_step(a, b)
                if place == 1 and midway is not None:
                    midway()
            self.whole_form()
            for step in range(FAST_REFINE):
                sizes = self.refine_step()
            self.rho[0:1] = self.rho[0:1] + functools.reduce(jnp.add, sizes)
            return
        scale = 1.0 / bound
        for e in self.energies:
            real = self.inv[e, 0] * scale
            imag = self.inv[e, 1] * scale
            self.inv[e, 0] = real
            self.inv[e, 1] = imag
        self.whole_form()

        def grow(carry):
            lowest, done = carry
            used = jnp.maximum(lowest, LEAST)
            a = 4.0 / (1.0 + used)
            b = a / (1.0 + used)
            after = jnp.minimum(lowest * (a - b * lowest), b * used)
            for e in self.energies:
                real, imag = product(self.inv_f.at[e], self.sys_f.at[e])
                store(self.tmp_f.at[e], real, imag)
            for e in self.energies:
                real, imag = product(self.tmp_f.at[e], self.inv_f.at[e])
                real = a * self.inv[e, 0] - b * real
                imag = a * self.inv[e, 1] - b * imag
                self.inv[e, 0] = real
                self.inv[e, 1] = imag
                store(self.inv_f.at[e], real, imag)
            return after, done + 1

        lax.while_loop(
            lambda carry: jnp.logical_and(carry[0] < 0.9, carry[1] < 64),
            grow,
            (broaden * broaden * scale, jnp.int32(0)),
        )

        def refine(carry):
            sizes = [jnp.sum(size) for size in self.refine_step()]
            return functools.reduce(jnp.maximum, sizes), carry[1] + 1

        lax.while_loop(
            lambda carry: jnp.logical_and(carry[0] > 4.0e-6, carry[1] < 24),
            refine,
            (jnp.float32(1.0), jnp.int32(0)),
        )

    def level(self, slab, last, midway=None):
        at_left = 0.0 if last else jnp.where(slab == 0, 1.0, 0.0)
        for e in self.energies:
            less = self.block(slab, 0, e)
            great = self.block(slab, 1, e)
            fill = self.scal(2, e) if last else at_left * self.scal(1, e)
            contact = contact_rate if last else at_left * contact_rate
            sys_r = self.scal(0, e) * self.eye - self.ham[slab, 0] - 0.5 * (great[0] - less[0])
            sys_i = (broaden + contact) * self.eye - self.ham[slab, 1] - 0.5 * (great[1] - less[1])
            inj_r = less[0]
            inj_i = less[1] + 2.0 * contact_rate * fill * self.eye
            if not last:
                sys_r = sys_r - self.folded_r[e, 0]
                sys_i = sys_i - self.folded_r[e, 1]
                inj_r = inj_r + self.folded_l[e, 0]
                inj_i = inj_i + self.folded_l[e, 1]
            store(self.sys_f.at[e], sys_r, sys_i)
            store(self.inj_f.at[e], inj_r, inj_i)
            back_r = sys_r.T
            back_i = -sys_i.T
            self.inv[e, 0] = back_r
            self.inv[e, 1] = back_i
            store_high(self.inv_f.at[e], back_r, back_i)
        self.invert(midway)
        for e in self.energies:
            self.gr[slab, e] = self.inv[e]
            self.gr_f[slab, e] = self.inv_f[e]
            real, imag = product(self.inv_f.at[e], self.inj_f.at[e])
            store(self.tmp_f.at[e], real, imag)
        for e in self.energies:
            real, imag = product(self.tmp_f.at[e], self.inv_f.at[e], dagger=True)
            self.gl[slab, e, 0] = real
            self.gl[slab, e, 1] = imag
            store(self.inj_f.at[e], real, imag)

    def fold(self, slab):
        for e in self.energies:
            real, imag = product(self.hop_f, self.gr_f.at[slab, e])
            store(self.t_f.at[slab, e], real, imag)
            real, imag = product(self.hop_f, self.inj_f.at[e])
            store(self.l_f.at[slab, e], real, imag)
        for e in self.energies:
            real, imag = product(self.t_f.at[slab, e], self.hop_f, dagger=True)
            self.folded_r[e, 0] = real
            self.folded_r[e, 1] = imag
            real, imag = product(self.l_f.at[slab, e], self.hop_f, dagger=True)
            self.folded_l[e, 0] = real
            self.folded_l[e, 1] = imag

    def flow(self):
        flow = jnp.zeros((1, W), F32)
        for e in self.energies:
            fill = self.scal(1, e)
            less = self.gl[0, e, 1]
            mixed = fill * (less + 2.0 * self.gr[0, e, 1]) + (1.0 - fill) * less
            flow = flow - jnp.sum(mixed * self.eye, axis=0, keepdims=True)
        flow = jnp.broadcast_to(jnp.sum(flow, axis=1, keepdims=True), (8, W))
        missed = jnp.broadcast_to(jnp.sum(self.rho[0:1], axis=1, keepdims=True), (8, W))
        missed = jnp.where(missed <= RESIDUAL, 0.0, 1.0)
        return jnp.where(lax.broadcasted_iota(jnp.int32, (8, W), 0) == 0, flow, missed)

    def finish(self, slab, e, green, less):
        self.less[e, slab, 0] = less[0]
        self.less[e, slab, 1] = less[1]
        self.great[e, slab, 0] = less[0] + green[0] - green[0].T
        self.great[e, slab, 1] = less[1] + green[1] + green[1].T
        store(self.full_f.at[0, e], *green)
        store(self.full_f.at[1, e], *less)

    def first(self):
        for e in self.energies:
            self.finish(0, e, (self.gr[0, e, 0], self.gr[0, e, 1]), (self.gl[0, e, 0], self.gl[0, e, 1]))

    def up(self, slab):
        for e in self.energies:
            real, imag = product(self.gr_f.at[slab, e], self.hop_f, dagger=True)
            store(self.sys_f.at[e], real, imag)
        for e in self.energies:
            real, imag = product(self.sys_f.at[e], self.full_f.at[0, e])
            store(self.tmp_f.at[e], real, imag)
            real, imag = product(self.sys_f.at[e], self.full_f.at[1, e])
            store(self.inj_f.at[e], real, imag)
        for e in self.energies:
            real, imag = product(self.tmp_f.at[e], self.t_f.at[slab, e])
            green = (self.gr[slab, e, 0] + real, self.gr[slab, e, 1] + imag)
            cross = product(self.tmp_f.at[e], self.l_f.at[slab, e])
            real, imag = product(self.inj_f.at[e], self.sys_f.at[e], dagger=True)
            less = (
                self.gl[slab, e, 0] + real + cross[0] - cross[0].T,
                self.gl[slab, e, 1] + imag + cross[1] + cross[1].T,
            )
            self.finish(slab, e, green, less)


def rows_of(sigma_ref):
    def read(slab, kind, e):
        return jnp.concatenate([sigma_ref[slab, owner, kind, e] for owner in range(sigma_ref.shape[1])], 0)

    return read


def sure_kernel(fast, scal_ref, sig_ref, ham_ref, hop_ref, less_ref, great_ref, flow_ref, *scratch):
    base = pl.program_id(0) * sig_ref.shape[3]
    solver = Solver(fast, rows_of(sig_ref), scal_ref, ham_ref, less_ref, great_ref, scratch, base)
    slabs = solver.slabs
    solver.start(hop_ref)
    solver.level(slabs - 1, True)

    def down(step, carry):
        slab = slabs - 2 - step
        solver.fold(slab + 1)
        solver.level(slab, False)
        return carry

    lax.fori_loop(0, slabs - 1, down, 0)
    flow_ref[0] = solver.flow()
    solver.first()

    def up(slab, carry):
        solver.up(slab)
        return carry

    lax.fori_loop(1, slabs, up, 0)


def transport(scalars, sigma, hamiltonian, coupling, fast=False):
    slabs, owners, _, count, depth = sigma.shape[:5]
    some = count if fast else 1
    vmem = pl.BlockSpec(memory_space=pltpu.VMEM)
    blocks = jax.ShapeDtypeStruct((count, slabs, 2, W, W), F32)
    out_spec = pl.BlockSpec((some, slabs, 2, W, W), lambda e: (e, 0, 0, 0, 0))
    less_new, great_new, flow = pl.pallas_call(
        functools.partial(sure_kernel, fast),
        grid=(count // some,),
        out_shape=(blocks, blocks, jax.ShapeDtypeStruct((count // some, 8, W), F32)),
        in_specs=[
            pl.BlockSpec(memory_space=pltpu.SMEM),
            pl.BlockSpec((slabs, owners, 2, some, depth, W), lambda e: (0, 0, 0, e, 0, 0)),
            vmem,
            vmem,
        ],
        out_specs=(out_spec, out_spec, pl.BlockSpec((1, 8, W), lambda e: (e, 0, 0))),
        scratch_shapes=Solver.scratch(some, slabs),
        compiler_params=pltpu.CompilerParams(vmem_limit_bytes=48 * 1024 * 1024),
        cost_estimate=pl.CostEstimate(flops=20_000_000_000, bytes_accessed=8_000_000, transcendentals=0),
    )(scalars, sigma, hamiltonian, coupling)
    return less_new, great_new, jnp.sum(flow, axis=0)


MESH = pl.DeviceIdType.MESH


def remote(source, target, send_sem, recv_sem, peer):
    return pltpu.make_async_remote_copy(
        src_ref=source, dst_ref=target, send_sem=send_sem, recv_sem=recv_sem,
        device_id=peer, device_id_type=MESH,
    )


def exchange_kernel(
    by, n_energy, n_mom,
    weight_ref, less_ref, great_ref, sigma_ref,
    pack, near_a, near_b, half_a, half_b, share, high, low, send_sem, recv_sem,
):
    place = lax.axis_index("energy")
    me = lax.axis_index("mom")
    count, slabs = less_ref.shape[:2]
    depth = W // n_mom
    after = lax.rem(me + 1, n_mom)
    before = lax.rem(me + n_mom - 1, n_mom)
    across = lax.rem(me + 2, n_mom)
    over = {"energy": lax.rem(place + by, n_energy)}
    under = {"energy": lax.rem(place - by + n_energy, n_energy)}
    wrapped_up = lax.div(place + by, n_energy)
    wrapped_down = 1 - lax.div(place - by + n_energy, n_energy)
    kept_up = (1 - wrapped_up).astype(F32)
    kept_down = (1 - wrapped_down).astype(F32)
    emission = weight_ref[0] * (1.0 / n_mom)
    absorption = weight_ref[1] * (1.0 / n_mom)

    barrier = pltpu.get_barrier_semaphore()
    for peer in ({"mom": after}, {"mom": before}, over, under):
        pl.semaphore_signal(barrier, inc=1, device_id=peer, device_id_type=MESH)

    def send(kind, chunk, source, target, peer):
        copy = remote(source, target, send_sem.at[kind, chunk], recv_sem.at[kind, chunk], peer)
        copy.start()
        return copy

    sent = {}
    rows = lax.broadcasted_iota(jnp.int32, (depth, W), 0)
    cols = lax.broadcasted_iota(jnp.int32, (depth, W), 1)
    order = range(slabs - 1, -1, -1)
    for c in order:
        for part in range(n_mom):
            span = slice(part * depth, (part + 1) * depth)
            upper = cols > rows + part * depth
            for kind, ref in enumerate((less_ref, great_ref)):
                pack[c, part, kind] = jnp.where(upper, ref[:, c, 0, span], ref[:, c, 1, span])
        if c == slabs - 1:
            pl.semaphore_wait(barrier, 4)
        sent[0, c] = send(0, c, pack.at[c, across, 0], near_a.at[c], {"mom": after})
        sent[1, c] = send(1, c, pack.at[c, across, 1], near_b.at[c], {"mom": before})
    for c in order:
        sent[0, c].wait_recv()
        pack[c, after, 0] = pack[c, after, 0] + near_a[c]
        sent[1, c].wait_recv()
        pack[c, before, 1] = pack[c, before, 1] + near_b[c]
        sent[2, c] = send(2, c, pack.at[c, after], half_a.at[c], {"mom": after})
        sent[3, c] = send(3, c, pack.at[c, before], half_b.at[c], {"mom": before})
    for c in order:
        sent[2, c].wait_recv()
        sent[3, c].wait_recv()
        share[c] = pack[c, me] + (half_a[c] + half_b[c])
        sent[4, c] = send(4, c, share.at[c], high.at[c], under)
        sent[5, c] = send(5, c, share.at[c], low.at[c], over)
    for c in order:
        sent[4, c].wait_recv()
        sent[5, c].wait_recv()
        for j in range(count):
            if j < count - 1:
                up = [high[c, kind, j + wrapped_up] for kind in range(2)]
            else:
                up = [high[c, kind, j] * kept_up for kind in range(2)]
            if j > 0:
                down = [low[c, kind, j - wrapped_down] for kind in range(2)]
            else:
                down = [low[c, kind, j] * kept_down for kind in range(2)]
            sigma_ref[c, 0, j] = emission * up[0] + absorption * down[0]
            sigma_ref[c, 1, j] = emission * down[1] + absorption * up[1]
    for copy in sent.values():
        copy.wait_send()


def exchange(by, n_energy, n_mom, weight, lesser, greater):
    count, slabs = lesser.shape[:2]
    depth = W // n_mom
    vmem = pl.BlockSpec(memory_space=pltpu.VMEM)
    half = pltpu.VMEM((slabs, count, depth, W), F32)
    whole = pltpu.VMEM((slabs, 2, count, depth, W), F32)
    return pl.pallas_call(
        functools.partial(exchange_kernel, by, n_energy, n_mom),
        out_shape=jax.ShapeDtypeStruct((slabs, 2, count, depth, W), F32),
        in_specs=[pl.BlockSpec(memory_space=pltpu.SMEM), vmem, vmem],
        out_specs=vmem,
        scratch_shapes=[
            pltpu.VMEM((slabs, n_mom, 2, count, depth, W), F32),
            half, half, whole, whole, whole, whole, whole,
            pltpu.SemaphoreType.DMA((6, slabs)),
            pltpu.SemaphoreType.DMA((6, slabs)),
        ],
        compiler_params=pltpu.CompilerParams(
            collective_id=by, has_side_effects=True, vmem_limit_bytes=32 * 1024 * 1024
        ),
    )(weight, lesser, greater)


def fast_kernel(
    n_mom, inner, outer,
    scal_ref, share_ref, ham_ref, hop_ref, less_ref, great_ref, total_ref,
    sigma, first, second, tile, partial, send_sem, recv_sem, sum_send, sum_recv, *scratch,
):
    solver = Solver(True, rows_of(sigma), scal_ref, ham_ref, less_ref, great_ref, scratch)
    slabs = solver.slabs
    place = lax.axis_index("energy")
    me = lax.axis_index("mom")
    after = lax.rem(me + 1, n_mom)
    before = lax.rem(me + n_mom - 1, n_mom)
    low = lax.rem(place, inner)
    high = lax.div(place, inner)
    slot = high * n_mom + me

    def outer_peer(step):
        other = lax.rem(slot + step, outer)
        return other, {"energy": lax.div(other, n_mom) * inner + low, "mom": lax.rem(other, n_mom)}

    def inner_peer(step):
        other = lax.rem(low + step, inner)
        return other, {"energy": high * inner + other, "mom": me}

    barrier = pltpu.get_barrier_semaphore()
    for step in range(1, outer):
        pl.semaphore_signal(barrier, inc=1, device_id=outer_peer(step)[1], device_id_type=MESH)
    for step in range(1, inner):
        pl.semaphore_signal(barrier, inc=1, device_id=inner_peer(step)[1], device_id_type=MESH)

    def near(slab):
        for kind, peer in ((0, after), (1, before)):
            yield remote(
                share_ref.at[slab], sigma.at[slab, me],
                send_sem.at[kind, slab], recv_sem.at[kind, slab], {"mom": peer},
            )

    def far(slab):
        for kind, owner, peer in ((0, before, after), (1, after, before)):
            part = sigma.at[slab, owner, kind]
            yield remote(
                part, part, send_sem.at[2 + kind, slab], recv_sem.at[2 + kind, slab], {"mom": peer}
            )

    def started(copies):
        for copy in copies:
            copy.start()

    def arrived(copies):
        for copy in copies:
            copy.wait_recv()

    rest = range(slabs - 2, -1, -1)
    solver.start(hop_ref)
    for slab in range(slabs):
        sigma[slab, me] = share_ref[slab]
    pl.semaphore_wait(barrier, outer + inner - 2)
    started(near(slabs - 1))
    arrived(near(slabs - 1))
    started(far(slabs - 1))
    for slab in rest:
        started(near(slab))
    arrived(far(slabs - 1))

    def midway():
        for slab in rest:
            arrived(near(slab))
            started(far(slab))

    solver.level(slabs - 1, True, midway)

    def down(step, carry):
        slab = slabs - 2 - step
        solver.fold(slab + 1)
        arrived(far(slab))
        solver.level(slab, False)
        return carry

    lax.fori_loop(0, slabs - 1, down, 0)

    def round_of(source, slots, size, own, peer, base):
        def copy(index, step):
            return remote(
                source, slots.at[index], sum_send.at[base + step], sum_recv.at[base + index], peer(step)[1]
            )

        def begin():
            for step in range(1, size):
                copy(own, step).start()
            slots[own] = source[...]

        def end():
            for step in range(1, size):
                copy(peer(step)[0], step).wait_recv()
            result = slots[0]
            for index in range(1, size):
                result = result + slots[index]
            for step in range(1, size):
                copy(own, step).wait_send()
            return result

        return begin, end

    begin_outer, end_outer = round_of(tile, first, outer, slot, outer_peer, 0)
    begin_inner, end_inner = round_of(partial, second, inner, low, inner_peer, outer)
    tile[...] = solver.flow()
    solver.first()
    begin_outer()
    solver.up(1)
    partial[...] = end_outer()
    solver.up(2)
    begin_inner()
    for slab in range(3, slabs):
        solver.up(slab)
    total_ref[...] = end_inner()
    for slab in range(slabs):
        for copies in (near(slab), far(slab)):
            for copy in copies:
                copy.wait_send()


def quick(n_energy, n_mom, scalars, share, hamiltonian, coupling, inner=8):
    slabs, _, count, depth = share.shape[:4]
    outer = n_energy // inner * n_mom
    vmem = pl.BlockSpec(memory_space=pltpu.VMEM)
    blocks = jax.ShapeDtypeStruct((count, slabs, 2, W, W), F32)
    return pl.pallas_call(
        functools.partial(fast_kernel, n_mom, inner, outer),
        out_shape=(blocks, blocks, jax.ShapeDtypeStruct((8, W), F32)),
        in_specs=[pl.BlockSpec(memory_space=pltpu.SMEM), vmem, vmem, vmem],
        out_specs=(vmem, vmem, vmem),
        scratch_shapes=[
            pltpu.VMEM((slabs, n_mom, 2, count, depth, W), F32),
            pltpu.VMEM((outer, 8, W), F32),
            pltpu.VMEM((inner, 8, W), F32),
            pltpu.VMEM((8, W), F32),
            pltpu.VMEM((8, W), F32),
            pltpu.SemaphoreType.DMA((4, slabs)),
            pltpu.SemaphoreType.DMA((4, slabs)),
            pltpu.SemaphoreType.DMA((outer + inner,)),
            pltpu.SemaphoreType.DMA((outer + inner,)),
        ]
        + Solver.scratch(count, slabs),
        compiler_params=pltpu.CompilerParams(
            collective_id=SMAX + 1, has_side_effects=True, vmem_limit_bytes=48 * 1024 * 1024
        ),
    )(scalars, share, hamiltonian, coupling)


def shards(lesser, greater, hamiltonian, coupling, shift, phonon_weight):
    n_energy = lax.axis_size("energy")
    n_mom = lax.axis_size("mom")
    here = lax.axis_index("energy")
    count = lesser.shape[0]
    total = count * n_energy
    branches = [functools.partial(exchange, k + 1, n_energy, n_mom) for k in range(SMAX)]
    share = lax.switch(shift[0] - 1, branches, phonon_weight, lesser[:, 0, 0], greater[:, 0, 0])
    grid = (jnp.arange(count) * n_energy + here).astype(F32)
    energy = (grid + 0.5) * (2.0 * band_edge / total) - band_edge
    scalars = jnp.stack(
        [
            energy,
            jax.nn.sigmoid((left_level - energy) / thermal),
            jax.nn.sigmoid((right_level - energy) / thermal),
        ]
    )
    ham, hop = hamiltonian[0], coupling[0]
    less_new, great_new, tile = quick(n_energy, n_mom, scalars, share, ham, hop)

    def again(share, less_new, great_new, flow):
        sigma = jnp.swapaxes(lax.all_gather(share, "mom", axis=0), 0, 1)
        less_new, great_new, tile = transport(scalars, sigma, ham, hop)
        return less_new, great_new, lax.psum(tile[0, 0], ("energy", "mom"))

    def keep(share, less_new, great_new, flow):
        return less_new, great_new, flow

    less_new, great_new, flow = lax.cond(
        tile[1, 0] > 0.5, again, keep, share, less_new, great_new, tile[0, 0]
    )
    current = flow * (2.0 * band_edge / total)
    return (less_new[:, None, None], great_new[:, None, None], current)


def solution(mesh):
    return jax.shard_map(
        shards,
        mesh=mesh,
        in_specs=(
            P(None, "energy", "mom", None, None, None, None),
            P(None, "energy", "mom", None, None, None, None),
            P("mom", None, None, None, None),
            P("mom", None, None, None),
            P(),
            P(),
        ),
        out_specs=(
            P(None, "energy", "mom", None, None, None, None),
            P(None, "energy", "mom", None, None, None, None),
            P(),
        ),
        check_vma=False,
    )
```

time: 107 us -> 113 us (1.056); the launches traced: 109 us -> 112 us
  Pallas kernels: 104 us -> 89.3 us
  between operations: 3.12 us -> 16.5 us
  local copies, waits for them, and re-layouts: 1.78 us -> 5.5 us
    pallas_call x1, Pallas kernels: 52.8 us -> 33.5 us  [exchange(): pl.pallas_call(functools.partial(exchange_kernel, by, n_energy, n_mom), o...]
    pallas_call x2 -> x1, Pallas kernels: 50.8 us -> 55.8 us  [quick(): pl.pallas_call(functools.partial(fast_kernel, n_mom, inner, outer), out_s...]
    unnamed x6, local copies, waits for them, and re-layouts: 0.6 us -> 4.47 us
where the time goes in v3:
time: 113 us; the launch traced here: 112 us
  Pallas kernels  89.3 us (79%)
  between operations  16.5 us (15%)
  local copies, waits for them, and re-layouts  5.5 us (5%)
    pallas_call x1, Pallas kernels, quick(): pl.pallas_call(functools.partial(fast_kernel, n_mom, inner, outer), out_s...  55.8 us
    pallas_call x1, Pallas kernels, exchange(): pl.pallas_call(functools.partial(exchange_kernel, by, n_energy, n_mom), o...  33.5 us
    unnamed x6, local copies, waits for them, and re-layouts  4.47 us

profile of v3, /device:TPU:1, one launch (start us, length us, event | category | flops | bytes accessed | tf_op | source)
XLA Modules:
  0.0 112.1 jit_solution(9365838535056661715)
XLA Ops:
  7.9 0.0 copy-start.1
  7.9 0.0 copy-start.2
  7.9 33.6 %conditional.2 = (f32[4,2,4,32,128]{4,3,2,1,0:T(8,128)S(1)}) conditional(s32[]{:T(128)} %bitcast.4, (f32[2]{0:T(128)}, f32[4,4,2,128,128]{4,3,2,1,0:T(8,128)}, f32[4,4,2,128,128]{4,3,2,1,0:T(8,128)}) %tuple.67, (f32[2]{0:T(128)}, f32[4,4,2,128,128]{4,3,2,1,0:T(8,128)}, f32[4,4,2,128,128]{4,3,2,1,0:T(8,128)}) %tuple.68, ...), branch_computations={%region_0.0_spmd, %region_1.0_spmd, %region_2.0_spmd, %region_3.0_... | conditional | bytes 8 | solution.py:641
  7.9 33.5 %branch_5_fun.1 = f32[4,2,4,32,128]{4,3,2,1,0:T(8,128)S(1)} custom-call(f32[2]{0:T(128)} %get-tuple-element.87.weight_ref, f32[4,4,2,128,128]{4,3,2,1,0:T(8,128)} %get-tuple-element.88.less_ref, f32[4,4,2,128,128]{4,3,2,1,0:T(8,128)} %get-tuple-element.89.great_ref), custom_call_target="tpu_custom_call" | custom-call | tf_op jit(solution)/shard_map/cond/branch_5_fun/pallas_call | solution.py:469
  41.5 0.0 copy-done.1
  41.5 0.0 copy-done.2
  41.5 55.8 %shard_map.85 = (f32[4,4,2,128,128]{4,3,2,1,0:T(8,128)S(1)}, f32[4,4,2,128,128]{4,3,2,1,0:T(8,128)}, f32[8,128]{1,0:T(8,128)S(1)}) custom-call(f32[3,4]{1,0:T(4,128)S(1)} %pad_maximum_fusion.scal_ref, f32[4,2,4,32,128]{4,3,2,1,0:T(8,128)S(1)} %get-tuple-element.125.share_ref, f32[4,2,128,128]{3,2,1,0:T(8,128)S(1)} %bitcast.31, f32[2,128,128]{2,1,0:T(8,128)S(1)} %bitcast.33), custom_call_target="tpu_custom_call" | custom-call | tf_op jit(solution)/shard_map/pallas_call | solution.py:611
  97.3 0.5 slice.10
  98.5 1.2 %conditional.3 = (f32[]{:T(128)}, f32[4,4,2,128,128]{4,3,2,1,0:T(8,128)S(1)}, f32[4,4,2,128,128]{4,3,2,1,0:T(8,128)}) conditional(s32[]{:T(128)} %bitcast.9, (f32[4,4,2,128,128]{4,3,2,1,0:T(8,128)S(1)}, f32[4,4,2,128,128]{4,3,2,1,0:T(8,128)}, f32[8,128]{1,0:T(8,128)S(1)}) %shard_map.85, (f32[4,2,4,32,128]{4,3,2,1,0:T(8,128)S(1)}, ...), branch_computations={%region_7.0_spmd, %region_8.0_spmd} | conditional | flops 20000002048 | bytes 22176380 | solution.py:662
  98.5 0.5 slice.7
  99.7 1.3 %copy.29 = f32[4,1,1,4,2,128,128]{6,5,4,3,2,1,0:T(8,128)} copy(f32[4,1,1,4,2,128,128]{6,5,4,3,2,1,0:T(8,128)S(1)} %bitcast.29) | data formatting | bytes 4194304
  101.0 3.1 %copy.30 = f32[4,1,1,4,2,128,128]{6,5,4,3,2,1,0:T(8,128)} copy(f32[4,1,1,4,2,128,128]{6,5,4,3,2,1,0:T(8,128)} %bitcast.11) | data formatting | bytes 4194304
  (3 shorter events, 0.0 us)
Async XLA Ops:
  7.9 33.6 %copy-start.1 = (f32[1,4,2,128,128]{4,3,2,1,0:T(8,128)S(1)}, f32[1,4,2,128,128]{4,3,2,1,0:T(8,128)}, u32[]{:S(2)}) copy-start(f32[1,4,2,128,128]{4,3,2,1,0:T(8,128)} %param.17) | copy-start | bytes 1572868
  7.9 33.6 %copy-start.2 = (f32[1,2,128,128]{3,2,1,0:T(8,128)S(1)}, f32[1,2,128,128]{3,2,1,0:T(8,128)}, u32[]{:S(2)}) copy-start(f32[1,2,128,128]{3,2,1,0:T(8,128)} %param.18) | copy-start | bytes 393220

commit v4 on v3

--- a/solution.py
+++ b/solution.py
@@ -31,6 +31,13 @@
 def store_high(ref, real, imag):
     ref[:W, :W] = real.astype(BF)
     ref[W:, :W] = imag.astype(BF)
+
+
+def unpacked(value, rows, cols):
+    turned = value.T
+    real = jnp.where(rows < cols, value, jnp.where(rows > cols, -turned, 0.0))
+    imag = jnp.where(rows >= cols, value, turned)
+    return real, imag
 
 
 def product(left, right, dagger=False, high=False):
@@ -83,13 +90,12 @@
         "inv", "gl", "gr", "folded_r", "folded_l", "rho",
     )
 
-    def __init__(self, fast, sigma, scal, ham, less, great, scratch, base=0):
+    def __init__(self, fast, sigma, scal, ham, out, scratch, base=0):
         self.fast = fast
         self.sigma = sigma
         self.scal = lambda row, e: scal[row, base + e]
         self.ham = ham
-        self.less = less
-        self.great = great
+        self.out = out
         for name, ref in zip(self.names, scratch, strict=True):
             setattr(self, name, ref)
         self.count = self.inv.shape[0]
@@ -116,12 +122,8 @@
         store(self.hop_f, hop[0].T, -hop[1].T)
         self.rho[...] = jnp.zeros((8, W), F32)
 
-    def block(self, slab, kind, e):
-        value = self.sigma(slab, kind, e)
-        turned = value.T
-        real = jnp.where(self.rows < self.cols, value, jnp.where(self.rows > self.cols, -turned, 0.0))
-        imag = jnp.where(self.rows >= self.cols, value, turned)
-        return real, imag
+    def block(self, sigma, slab, kind, e):
+        return unpacked(sigma(slab, kind, e), self.rows, self.cols)
 
     def grow_step(self, a, b):
         for e in self.energies:
@@ -226,11 +228,12 @@
             (jnp.float32(1.0), jnp.int32(0)),
         )
 
-    def level(self, slab, last, midway=None):
+    def level(self, slab, last, midway=None, sigma=None):
+        sigma = self.sigma if sigma is None else sigma
         at_left = 0.0 if last else jnp.where(slab == 0, 1.0, 0.0)
         for e in self.energies:
-            less = self.block(slab, 0, e)
-            great = self.block(slab, 1, e)
+            less = self.block(sigma, slab, 0, e)
+            great = self.block(sigma, slab, 1, e)
             fill = self.scal(2, e) if last else at_left * self.scal(1, e)
             contact = contact_rate if last else at_left * contact_rate
             sys_r = self.scal(0, e) * self.eye - self.ham[slab, 0] - 0.5 * (great[0] - less[0])
@@ -288,10 +291,10 @@
         return jnp.where(lax.broadcasted_iota(jnp.int32, (8, W), 0) == 0, flow, missed)
 
     def finish(self, slab, e, green, less):
-        self.less[e, slab, 0] = less[0]
-        self.less[e, slab, 1] = less[1]
-        self.great[e, slab, 0] = less[0] + green[0] - green[0].T
-        self.great[e, slab, 1] = less[1] + green[1] + green[1].T
+        great = (less[0] + green[0] - green[0].T, less[1] + green[1] + green[1].T)
+        upper = self.rows < self.cols
+        self.out[e, slab, 0] = jnp.where(upper, less[0], less[1])
+        self.out[e, slab, 1] = jnp.where(upper, great[0], great[1])
         store(self.full_f.at[0, e], *green)
         store(self.full_f.at[1, e], *less)
 
@@ -327,9 +330,9 @@
     return read
 
 
-def sure_kernel(fast, scal_ref, sig_ref, ham_ref, hop_ref, less_ref, great_ref, flow_ref, *scratch):
+def sure_kernel(fast, scal_ref, sig_ref, ham_ref, hop_ref, out_ref, flow_ref, *scratch):
     base = pl.program_id(0) * sig_ref.shape[3]
-    solver = Solver(fast, rows_of(sig_ref), scal_ref, ham_ref, less_ref, great_ref, scratch, base)
+    solver = Solver(fast, rows_of(sig_ref), scal_ref, ham_ref, out_ref, scratch, base)
     slabs = solver.slabs
     solver.start(hop_ref)
     solver.level(slabs - 1, True)
@@ -357,25 +360,48 @@
     vmem = pl.BlockSpec(memory_space=pltpu.VMEM)
     blocks = jax.ShapeDtypeStruct((count, slabs, 2, W, W), F32)
     out_spec = pl.BlockSpec((some, slabs, 2, W, W), lambda e: (e, 0, 0, 0, 0))
-    less_new, great_new, flow = pl.pallas_call(
+    packed, flow = pl.pallas_call(
         functools.partial(sure_kernel, fast),
         grid=(count // some,),
-        out_shape=(blocks, blocks, jax.ShapeDtypeStruct((count // some, 8, W), F32)),
+        out_shape=(blocks, jax.ShapeDtypeStruct((count // some, 8, W), F32)),
         in_specs=[
             pl.BlockSpec(memory_space=pltpu.SMEM),
             pl.BlockSpec((slabs, owners, 2, some, depth, W), lambda e: (0, 0, 0, e, 0, 0)),
             vmem,
             vmem,
         ],
-        out_specs=(out_spec, out_spec, pl.BlockSpec((1, 8, W), lambda e: (e, 0, 0))),
+        out_specs=(out_spec, pl.BlockSpec((1, 8, W), lambda e: (e, 0, 0))),
         scratch_shapes=Solver.scratch(some, slabs),
-        compiler_params=pltpu.CompilerParams(vmem_limit_bytes=48 * 1024 * 1024),
+        compiler_params=pltpu.CompilerParams(vmem_limit_bytes=(44 if fast else 16) * 1024 * 1024),
         cost_estimate=pl.CostEstimate(flops=20_000_000_000, bytes_accessed=8_000_000, transcendentals=0),
     )(scalars, sigma, hamiltonian, coupling)
-    return less_new, great_new, jnp.sum(flow, axis=0)
+    return packed, jnp.sum(flow, axis=0)
+
+
+def spread_kernel(packed_ref, less_ref, great_ref):
+    rows = lax.broadcasted_iota(jnp.int32, (W, W), 0)
+    cols = lax.broadcasted_iota(jnp.int32, (W, W), 1)
+    for slab in range(packed_ref.shape[1]):
+        for kind, ref in enumerate((less_ref, great_ref)):
+            real, imag = unpacked(packed_ref[0, slab, kind], rows, cols)
+            ref[0, slab, 0] = real
+            ref[0, slab, 1] = imag
+
+
+def spread(packed):
+    spec = pl.BlockSpec((1,) + packed.shape[1:], lambda e: (e, 0, 0, 0, 0))
+    return pl.pallas_call(
+        spread_kernel,
+        grid=(packed.shape[0],),
+        out_shape=(jax.ShapeDtypeStruct(packed.shape, F32),) * 2,
+        in_specs=[spec],
+        out_specs=(spec, spec),
+        compiler_params=pltpu.CompilerParams(vmem_limit_bytes=16 * 1024 * 1024),
+    )(packed)
 
 
 MESH = pl.DeviceIdType.MESH
+GATHERED = 2
 
 
 def remote(source, target, send_sem, recv_sem, peer):
@@ -416,6 +442,15 @@
         return copy
 
     sent = {}
+
+    def pass_on(c):
+        sent[6, c].wait_recv()
+        part = sigma_ref.at[c, before, 0]
+        sent[8, c] = send(8, c, part, part, {"mom": after})
+        sent[7, c].wait_recv()
+        part = sigma_ref.at[c, after, 1]
+        sent[9, c] = send(9, c, part, part, {"mom": before})
+
     rows = lax.broadcasted_iota(jnp.int32, (depth, W), 0)
     cols = lax.broadcasted_iota(jnp.int32, (depth, W), 1)
     order = range(slabs - 1, -1, -1)
@@ -454,8 +489,18 @@
                 down = [low[c, kind, j - wrapped_down] for kind in range(2)]
             else:
                 down = [low[c, kind, j] * kept_down for kind in range(2)]
-            sigma_ref[c, 0, j] = emission * up[0] + absorption * down[0]
-            sigma_ref[c, 1, j] = emission * down[1] + absorption * up[1]
+            sigma_ref[c, me, 0, j] = emission * up[0] + absorption * down[0]
+            sigma_ref[c, me, 1, j] = emission * down[1] + absorption * up[1]
+        if c >= slabs - GATHERED:
+            mine = sigma_ref.at[c, me]
+            sent[6, c] = send(6, c, mine, mine, {"mom": after})
+            sent[7, c] = send(7, c, mine, mine, {"mom": before})
+        if c + 1 < slabs and c + 1 >= slabs - GATHERED:
+            pass_on(c + 1)
+    for c in order:
+        if (8, c) in sent:
+            sent[8, c].wait_recv()
+            sent[9, c].wait_recv()
     for copy in sent.values():
         copy.wait_send()
 
@@ -468,14 +513,14 @@
     whole = pltpu.VMEM((slabs, 2, count, depth, W), F32)
     return pl.pallas_call(
         functools.partial(exchange_kernel, by, n_energy, n_mom),
-        out_shape=jax.ShapeDtypeStruct((slabs, 2, count, depth, W), F32),
+        out_shape=jax.ShapeDtypeStruct((slabs, n_mom, 2, count, depth, W), F32),
         in_specs=[pl.BlockSpec(memory_space=pltpu.SMEM), vmem, vmem],
         out_specs=vmem,
         scratch_shapes=[
             pltpu.VMEM((slabs, n_mom, 2, count, depth, W), F32),
             half, half, whole, whole, whole, whole, whole,
-            pltpu.SemaphoreType.DMA((6, slabs)),
-            pltpu.SemaphoreType.DMA((6, slabs)),
+            pltpu.SemaphoreType.DMA((10, slabs)),
+            pltpu.SemaphoreType.DMA((10, slabs)),
         ],
         compiler_params=pltpu.CompilerParams(
             collective_id=by, has_side_effects=True, vmem_limit_bytes=32 * 1024 * 1024
@@ -485,10 +530,10 @@
 
 def fast_kernel(
     n_mom, inner, outer,
-    scal_ref, share_ref, ham_ref, hop_ref, less_ref, great_ref, total_ref,
+    scal_ref, share_ref, ham_ref, hop_ref, out_ref, total_ref,
     sigma, first, second, tile, partial, send_sem, recv_sem, sum_send, sum_recv, *scratch,
 ):
-    solver = Solver(True, rows_of(sigma), scal_ref, ham_ref, less_ref, great_ref, scratch)
+    solver = Solver(True, rows_of(sigma), scal_ref, ham_ref, out_ref, scratch)
     slabs = solver.slabs
     place = lax.axis_index("energy")
     me = lax.axis_index("mom")
@@ -515,7 +560,7 @@
     def near(slab):
         for kind, peer in ((0, after), (1, before)):
             yield remote(
-                share_ref.at[slab], sigma.at[slab, me],
+                share_ref.at[slab, me], sigma.at[slab, me],
                 send_sem.at[kind, slab], recv_sem.at[kind, slab], {"mom": peer},
             )
 
@@ -534,30 +579,36 @@
         for copy in copies:
             copy.wait_recv()
 
-    rest = range(slabs - 2, -1, -1)
+    rest = range(slabs - GATHERED - 1, -1, -1)
+
+    def share_rest():
+        pl.semaphore_wait(barrier, outer + inner - 2)
+        for slab in range(slabs - GATHERED, slabs - 1):
+            sigma[slab] = share_ref[slab]
+        for slab in rest:
+            started(near(slab))
+            sigma[slab, me] = share_ref[slab, me]
+
     solver.start(hop_ref)
-    for slab in range(slabs):
-        sigma[slab, me] = share_ref[slab]
-    pl.semaphore_wait(barrier, outer + inner - 2)
-    started(near(slabs - 1))
-    arrived(near(slabs - 1))
-    started(far(slabs - 1))
-    for slab in rest:
-        started(near(slab))
-    arrived(far(slabs - 1))
-
-    def midway():
-        for slab in rest:
-            arrived(near(slab))
-            started(far(slab))
-
-    solver.level(slabs - 1, True, midway)
+    solver.level(slabs - 1, True, share_rest, rows_of(share_ref))
 
     def down(step, carry):
         slab = slabs - 2 - step
+
+        def pass_on():
+            @pl.when(step == 0)
+            def _():
+                for other in rest:
+                    arrived(near(other))
+                    started(far(other))
+
         solver.fold(slab + 1)
-        arrived(far(slab))
-        solver.level(slab, False)
+
+        @pl.when(slab < slabs - GATHERED)
+        def _():
+            arrived(far(slab))
+
+        solver.level(slab, False, pass_on)
         return carry
 
     lax.fori_loop(0, slabs - 1, down, 0)
@@ -597,22 +648,22 @@
     for slab in range(3, slabs):
         solver.up(slab)
     total_ref[...] = end_inner()
-    for slab in range(slabs):
+    for slab in rest:
         for copies in (near(slab), far(slab)):
             for copy in copies:
                 copy.wait_send()
 
 
 def quick(n_energy, n_mom, scalars, share, hamiltonian, coupling, inner=8):
-    slabs, _, count, depth = share.shape[:4]
+    slabs, _, _, count, depth = share.shape[:5]
     outer = n_energy // inner * n_mom
     vmem = pl.BlockSpec(memory_space=pltpu.VMEM)
     blocks = jax.ShapeDtypeStruct((count, slabs, 2, W, W), F32)
     return pl.pallas_call(
         functools.partial(fast_kernel, n_mom, inner, outer),
-        out_shape=(blocks, blocks, jax.ShapeDtypeStruct((8, W), F32)),
+        out_shape=(blocks, jax.ShapeDtypeStruct((8, W), F32)),
         in_specs=[pl.BlockSpec(memory_space=pltpu.SMEM), vmem, vmem, vmem],
-        out_specs=(vmem, vmem, vmem),
+        out_specs=(vmem, vmem),
         scratch_shapes=[
             pltpu.VMEM((slabs, n_mom, 2, count, depth, W), F32),
             pltpu.VMEM((outer, 8, W), F32),
@@ -626,9 +677,14 @@
         ]
         + Solver.scratch(count, slabs),
         compiler_params=pltpu.CompilerParams(
-            collective_id=SMAX + 1, has_side_effects=True, vmem_limit_bytes=48 * 1024 * 1024
+            collective_id=SMAX + 1, has_side_effects=True, vmem_limit_bytes=26 * 1024 * 1024
         ),
     )(scalars, share, hamiltonian, coupling)
+
+
+def moved(array, axis, by):
+    size = lax.axis_size(axis)
+    return lax.ppermute(array, axis, [(i, (i + by) % size) for i in range(size)]) if by else array
 
 
 def shards(lesser, greater, hamiltonian, coupling, shift, phonon_weight):
@@ -649,19 +705,26 @@
         ]
     )
     ham, hop = hamiltonian[0], coupling[0]
-    less_new, great_new, tile = quick(n_energy, n_mom, scalars, share, ham, hop)
-
-    def again(share, less_new, great_new, flow):
-        sigma = jnp.swapaxes(lax.all_gather(share, "mom", axis=0), 0, 1)
-        less_new, great_new, tile = transport(scalars, sigma, ham, hop)
-        return less_new, great_new, lax.psum(tile[0, 0], ("energy", "mom"))
-
-    def keep(share, less_new, great_new, flow):
-        return less_new, great_new, flow
-
-    less_new, great_new, flow = lax.cond(
-        tile[1, 0] > 0.5, again, keep, share, less_new, great_new, tile[0, 0]
-    )
+    packed, tile = quick(n_energy, n_mom, scalars, share, ham, hop)
+
+    def again(share, packed, tile):
+        mine = share[:, lax.axis_index("mom")]
+        parts = jnp.stack([moved(mine, "mom", k) for k in range(n_mom)], 1)
+        owners = (lax.axis_index("mom") - jnp.arange(n_mom)) % n_mom
+        sigma = jnp.zeros_like(parts).at[:, owners].set(parts)
+        packed, tile = transport(scalars, sigma, ham, hop)
+        flow = tile[0, 0]
+        for axis, size in (("mom", n_mom), ("energy", n_energy)):
+            by = 1
+            while by < size:
+                flow = flow + lax.ppermute(flow, axis, [(i, i ^ by) for i in range(size)])
+                by = 2 * by
+        return (*spread(packed), flow)
+
+    def keep(share, packed, tile):
+        return (*spread(packed), tile[0, 0])
+
+    less_new, great_new, flow = lax.cond(tile[1, 0] > 0.5, again, keep, share, packed, tile)
     current = flow * (2.0 * band_edge / total)
     return (less_new[:, None, None], great_new[:, None, None], current)
 

time: 113 us -> 86.2 us (0.76)
  between operations: 16.5 us -> 3.13 us
  Pallas kernels: 89.3 us -> 81.1 us
  local copies, waits for them, and re-layouts: 5.5 us -> 1.04 us
    pallas_call x1, Pallas kernels: 55.8 us -> 40.4 us  [quick(): pl.pallas_call(functools.partial(fast_kernel, n_mom, inner, outer), out_s...]
    unnamed x6 -> x4, local copies, waits for them, and re-layouts: 4.47 us -> 0.01 us
    pallas_call x1, Pallas kernels: 33.5 us -> 37.9 us  [exchange(): pl.pallas_call(functools.partial(exchange_kernel, by, n_energy, n_mom), o...]
    pallas_call x0 -> x1, Pallas kernels: none -> 2.72 us  [spread(): pl.pallas_call(spread_kernel, grid=(packed.shape[0],), out_shape=(jax.Sha...]
where the time goes in v4:
time: 86.2 us; the launch traced here: 86 us
  Pallas kernels  81.1 us (94%)
  between operations  3.13 us (4%)
  local copies, waits for them, and re-layouts  1.04 us (1%)
    pallas_call x1, Pallas kernels, quick(): pl.pallas_call(functools.partial(fast_kernel, n_mom, inner, outer), out_s...  40.4 us
    pallas_call x1, Pallas kernels, exchange(): pl.pallas_call(functools.partial(exchange_kernel, by, n_energy, n_mom), o...  37.9 us
    pallas_call x1, Pallas kernels, spread(): pl.pallas_call(spread_kernel, grid=(packed.shape[0],), out_shape=(jax.Sha...  2.72 us

profile of v4, /device:TPU:1, one launch (start us, length us, event | category | flops | bytes accessed | tf_op | source)
XLA Modules:
  0.0 86.0 jit_solution(13968027365614371426)
XLA Ops:
  1.3 0.0 copy-start.2
  1.4 0.0 copy-start.3
  1.4 38.0 %conditional.2 = (f32[4,4,2,4,32,128]{5,4,3,2,1,0:T(8,128)S(1)}) conditional(s32[]{:T(128)} %bitcast.8, (f32[2]{0:T(128)}, f32[4,4,2,128,128]{4,3,2,1,0:T(8,128)}, f32[4,4,2,128,128]{4,3,2,1,0:T(8,128)}) %tuple.59, (f32[2]{0:T(128)}, f32[4,4,2,128,128]{4,3,2,1,0:T(8,128)}, ...), branch_computations={%region_0.0_spmd, %region_1.0_spmd, %region_2.0_spmd, %region_3.0_... | conditional | bytes 8 | solution.py:697
  1.4 37.9 %branch_1_fun.3 = f32[4,4,2,4,32,128]{5,4,3,2,1,0:T(8,128)S(1)} custom-call(f32[2]{0:T(128)} %get-tuple-element.62.weight_ref, f32[4,4,2,128,128]{4,3,2,1,0:T(8,128)} %get-tuple-element.63.less_ref, f32[4,4,2,128,128]{4,3,2,1,0:T(8,128)} %get-tuple-element.68.great_ref), custom_call_target="tpu_custom_call" | custom-call | tf_op jit(solution)/shard_map/cond/branch_1_fun/pallas_call | solution.py:514
  39.4 0.0 copy-done.2
  39.4 0.0 copy-done.3
  39.4 40.4 %shard_map.85 = (f32[4,4,2,128,128]{4,3,2,1,0:T(8,128)S(1)}, f32[8,128]{1,0:T(8,128)S(1)}) custom-call(f32[3,4]{1,0:T(4,128)S(1)} %pad_maximum_fusion.scal_ref, f32[4,4,2,4,32,128]{5,4,3,2,1,0:T(8,128)S(1)} %get-tuple-element.119.share_ref, f32[4,2,128,128]{3,2,1,0:T(8,128)S(1)} %bitcast.34, f32[2,128,128]{2,1,0:T(8,128)S(1)} %bitcast.39), custom_call_target="tpu_custom_call" | custom-call | tf_op jit(solution)/shard_map/pallas_call | solution.py:662
  79.8 0.5 slice.9
  81.0 3.9 %conditional.3 = (f32[4,4,2,128,128]{4,3,2,1,0:T(8,128)}, f32[4,4,2,128,128]{4,3,2,1,0:T(8,128)}, f32[]{:T(128)}) conditional(s32[]{:T(128)} %bitcast.13, (f32[4,4,2,128,128]{4,3,2,1,0:T(8,128)S(1)}, f32[8,128]{1,0:T(8,128)S(1)}) %shard_map.85, (f32[4,4,2,4,32,128]{5,4,3,2,1,0:T(8,128)S(1)}, f32[3,4]{1,0:T(4,128)S(1)}, ...), branch_computations={%region_7.0_spmd, %region_8.11_spmd} | conditional | flops 20001574912 | bytes 45770016 | solution.py:727
  81.0 0.5 slice.6
  82.2 2.7 %branch_0_fun.3 = (f32[4,4,2,128,128]{4,3,2,1,0:T(8,128)}, f32[4,4,2,128,128]{4,3,2,1,0:T(8,128)}) custom-call(f32[4,4,2,128,128]{4,3,2,1,0:T(8,128)S(1)} %get-tuple-element.84.packed_ref), custom_call_target="tpu_custom_call" | custom-call | tf_op jit(solution)/shard_map/cond/branch_0_fun/pallas_call | solution.py:393
  (3 shorter events, 0.0 us)
Async XLA Ops:
  1.3 38.0 %copy-start.2 = (f32[1,4,2,128,128]{4,3,2,1,0:T(8,128)S(1)}, f32[1,4,2,128,128]{4,3,2,1,0:T(8,128)}, u32[]{:S(2)}) copy-start(f32[1,4,2,128,128]{4,3,2,1,0:T(8,128)} %param.17) | copy-start | bytes 1572868
  1.4 38.0 %copy-start.3 = (f32[1,2,128,128]{3,2,1,0:T(8,128)S(1)}, f32[1,2,128,128]{3,2,1,0:T(8,128)}, u32[]{:S(2)}) copy-start(f32[1,2,128,128]{3,2,1,0:T(8,128)} %param.18) | copy-start | bytes 393220

commit v5 on v4

--- a/solution.py
+++ b/solution.py
@@ -8,6 +8,7 @@
 from jax.sharding import PartitionSpec as P
 
 SMAX = 7
+POINTS = 128
 broaden = 0.2
 contact_rate = 0.5
 left_level = 0.3
@@ -41,28 +42,28 @@
 
 
 def product(left, right, dagger=False, high=False):
-    if high:
-        lhs = left[:, :W]
-    else:
-        whole = left[...]
-        lhs = jnp.concatenate([whole, whole], 1)
     if dagger:
         up = right[:, :W]
-        low = None if high else right[:, W:]
-        rhs = up if high else jnp.concatenate([up, up, low, low], 1)
         dims = (((1,), (1,)), ((), ()))
     else:
         up = jnp.concatenate([right[:W, :W], right[W:, :W]], 1)
-        if high:
-            rhs = up
-        else:
-            low = jnp.concatenate([right[:W, W:], right[W:, W:]], 1)
-            rhs = jnp.concatenate([up, up, low, low], 0)
         dims = (((1,), (0,)), ((), ()))
+    if high:
+        lhs, rhs = left[:, :W], up
+    else:
+        lhs, rhs = left[...], jnp.concatenate([up, up], 1 if dagger else 0)
     full = lax.dot_general(lhs, rhs, dims, preferred_element_type=F32)
     if dagger:
-        return full[:W, :W] + full[W:, W:], full[W:, :W] - full[:W, W:]
-    return full[:W, :W] - full[W:, W:], full[:W, W:] + full[W:, :W]
+        real, imag = full[:W, :W] + full[W:, W:], full[W:, :W] - full[:W, W:]
+    else:
+        real, imag = full[:W, :W] - full[W:, W:], full[:W, W:] + full[W:, :W]
+    if high:
+        return real, imag
+    lhs = jnp.concatenate([left[:W, :W], left[W:, :W]], 1)
+    low_r, low_i = right[:W, W:], right[W:, W:]
+    rhs = jnp.concatenate([jnp.concatenate([low_r, low_i], 1), jnp.concatenate([-low_i, low_r], 1)], 0)
+    rest = lax.dot_general(lhs, rhs, dims, preferred_element_type=F32)
+    return real + rest[:, :W], imag + rest[:, W:]
 
 
 FAST_LOW = 0.006
@@ -99,6 +100,7 @@
         for name, ref in zip(self.names, scratch, strict=True):
             setattr(self, name, ref)
         self.count = self.inv.shape[0]
+        self.weight = 2.0 * band_edge / POINTS
         self.slabs = ham.shape[0]
         self.energies = range(self.count)
         self.rows = lax.broadcasted_iota(jnp.int32, (W, W), 0)
@@ -285,7 +287,7 @@
             less = self.gl[0, e, 1]
             mixed = fill * (less + 2.0 * self.gr[0, e, 1]) + (1.0 - fill) * less
             flow = flow - jnp.sum(mixed * self.eye, axis=0, keepdims=True)
-        flow = jnp.broadcast_to(jnp.sum(flow, axis=1, keepdims=True), (8, W))
+        flow = jnp.broadcast_to(jnp.sum(flow, axis=1, keepdims=True) * self.weight, (8, W))
         missed = jnp.broadcast_to(jnp.sum(self.rho[0:1], axis=1, keepdims=True), (8, W))
         missed = jnp.where(missed <= RESIDUAL, 0.0, 1.0)
         return jnp.where(lax.broadcasted_iota(jnp.int32, (8, W), 0) == 0, flow, missed)
@@ -413,13 +415,23 @@
 
 def exchange_kernel(
     by, n_energy, n_mom,
-    weight_ref, less_ref, great_ref, sigma_ref,
-    pack, near_a, near_b, half_a, half_b, share, high, low, send_sem, recv_sem,
+    weight_ref, less_hbm, great_hbm, sigma_ref,
+    less_ref, great_ref, load_sem, pack, near_a, near_b, half_a, half_b, share, high, low, send_sem, recv_sem,
 ):
     place = lax.axis_index("energy")
     me = lax.axis_index("mom")
-    count, slabs = less_ref.shape[:2]
+    slabs, count = less_ref.shape[:2]
     depth = W // n_mom
+    loads = [
+        [
+            pltpu.make_async_copy(source.at[:, c], target.at[c], load_sem.at[kind, c])
+            for kind, (source, target) in enumerate(((less_hbm, less_ref), (great_hbm, great_ref)))
+        ]
+        for c in range(slabs)
+    ]
+    for c in range(slabs - 1, -1, -1):
+        for load in loads[c]:
+            load.start()
     after = lax.rem(me + 1, n_mom)
     before = lax.rem(me + n_mom - 1, n_mom)
     across = lax.rem(me + 2, n_mom)
@@ -455,11 +467,13 @@
     cols = lax.broadcasted_iota(jnp.int32, (depth, W), 1)
     order = range(slabs - 1, -1, -1)
     for c in order:
+        for load in loads[c]:
+            load.wait()
         for part in range(n_mom):
             span = slice(part * depth, (part + 1) * depth)
             upper = cols > rows + part * depth
             for kind, ref in enumerate((less_ref, great_ref)):
-                pack[c, part, kind] = jnp.where(upper, ref[:, c, 0, span], ref[:, c, 1, span])
+                pack[c, part, kind] = jnp.where(upper, ref[c, :, 0, span], ref[c, :, 1, span])
         if c == slabs - 1:
             pl.semaphore_wait(barrier, 4)
         sent[0, c] = send(0, c, pack.at[c, across, 0], near_a.at[c], {"mom": after})
@@ -509,14 +523,17 @@
     count, slabs = lesser.shape[:2]
     depth = W // n_mom
     vmem = pl.BlockSpec(memory_space=pltpu.VMEM)
+    hbm = pl.BlockSpec(memory_space=pl.ANY)
+    block = pltpu.VMEM((slabs, count, 2, W, W), F32)
     half = pltpu.VMEM((slabs, count, depth, W), F32)
     whole = pltpu.VMEM((slabs, 2, count, depth, W), F32)
     return pl.pallas_call(
         functools.partial(exchange_kernel, by, n_energy, n_mom),
         out_shape=jax.ShapeDtypeStruct((slabs, n_mom, 2, count, depth, W), F32),
-        in_specs=[pl.BlockSpec(memory_space=pltpu.SMEM), vmem, vmem],
+        in_specs=[pl.BlockSpec(memory_space=pltpu.SMEM), hbm, hbm],
         out_specs=vmem,
         scratch_shapes=[
+            block, block, pltpu.SemaphoreType.DMA((2, slabs)),
             pltpu.VMEM((slabs, n_mom, 2, count, depth, W), F32),
             half, half, whole, whole, whole, whole, whole,
             pltpu.SemaphoreType.DMA((10, slabs)),
@@ -530,7 +547,7 @@
 
 def fast_kernel(
     n_mom, inner, outer,
-    scal_ref, share_ref, ham_ref, hop_ref, out_ref, total_ref,
+    scal_ref, share_ref, ham_ref, hop_ref, out_ref, flow_ref, missed_ref,
     sigma, first, second, tile, partial, send_sem, recv_sem, sum_send, sum_recv, *scratch,
 ):
     solver = Solver(True, rows_of(sigma), scal_ref, ham_ref, out_ref, scratch)
@@ -641,13 +658,14 @@
     tile[...] = solver.flow()
     solver.first()
     begin_outer()
-    solver.up(1)
+    for slab in range(1, slabs - 1):
+        solver.up(slab)
     partial[...] = end_outer()
-    solver.up(2)
     begin_inner()
-    for slab in range(3, slabs):
-        solver.up(slab)
-    total_ref[...] = end_inner()
+    solver.up(slabs - 1)
+    total = end_inner()
+    flow_ref[...] = total[0:1, 0:1]
+    missed_ref[...] = jnp.where(total[1:2, 0:1] > 0.5, 1, 0)
     for slab in rest:
         for copies in (near(slab), far(slab)):
             for copy in copies:
@@ -661,9 +679,13 @@
     blocks = jax.ShapeDtypeStruct((count, slabs, 2, W, W), F32)
     return pl.pallas_call(
         functools.partial(fast_kernel, n_mom, inner, outer),
-        out_shape=(blocks, jax.ShapeDtypeStruct((8, W), F32)),
+        out_shape=(
+            blocks,
+            jax.ShapeDtypeStruct((1, 1), F32),
+            jax.ShapeDtypeStruct((1, 1), jnp.int32),
+        ),
         in_specs=[pl.BlockSpec(memory_space=pltpu.SMEM), vmem, vmem, vmem],
-        out_specs=(vmem, vmem),
+        out_specs=(vmem, vmem, vmem),
         scratch_shapes=[
             pltpu.VMEM((slabs, n_mom, 2, count, depth, W), F32),
             pltpu.VMEM((outer, 8, W), F32),
@@ -705,9 +727,9 @@
         ]
     )
     ham, hop = hamiltonian[0], coupling[0]
-    packed, tile = quick(n_energy, n_mom, scalars, share, ham, hop)
-
-    def again(share, packed, tile):
+    packed, flow, missed = quick(n_energy, n_mom, scalars, share, ham, hop)
+
+    def again(share, packed, flow):
         mine = share[:, lax.axis_index("mom")]
         parts = jnp.stack([moved(mine, "mom", k) for k in range(n_mom)], 1)
         owners = (lax.axis_index("mom") - jnp.arange(n_mom)) % n_mom
@@ -721,11 +743,11 @@
                 by = 2 * by
         return (*spread(packed), flow)
 
-    def keep(share, packed, tile):
-        return (*spread(packed), tile[0, 0])
-
-    less_new, great_new, flow = lax.cond(tile[1, 0] > 0.5, again, keep, share, packed, tile)
-    current = flow * (2.0 * band_edge / total)
+    def keep(share, packed, flow):
+        return (*spread(packed), flow.reshape(()))
+
+    branch = missed.reshape(())
+    less_new, great_new, current = lax.switch(branch, [keep, again], share, packed, flow)
     return (less_new[:, None, None], great_new[:, None, None], current)
 
 

time: 86.2 us -> 82.8 us (0.961); the launches traced: 86 us -> 84.1 us
  local copies, waits for them, and re-layouts: 1.04 us -> 0.01 us
    pallas_call x1, Pallas kernels: 40.4 us -> 35.8 us  [quick(): pl.pallas_call(functools.partial(fast_kernel, n_mom, inner, outer), out_s...]
    pallas_call x1, Pallas kernels: 37.9 us -> 41.7 us  [exchange(): pl.pallas_call(functools.partial(exchange_kernel, by, n_energy, n_mom), o...]
    slice x2 -> x0, local copies, waits for them, and re-layouts: 1.03 us -> none  [the longest x1 0.51 us: shards(): tile[1, 0] > 0.5]
where the time goes in v5:
time: 82.8 us; the launch traced here: 84.1 us
  Pallas kernels  80.3 us (97%)
  between operations  3.74 us (5%)
    pallas_call x1, Pallas kernels, exchange(): pl.pallas_call(functools.partial(exchange_kernel, by, n_energy, n_mom), o...  41.7 us
    pallas_call x1, Pallas kernels, quick(): pl.pallas_call(functools.partial(fast_kernel, n_mom, inner, outer), out_s...  35.8 us
    pallas_call x1, Pallas kernels, spread(): pl.pallas_call(spread_kernel, grid=(packed.shape[0],), out_shape=(jax.Sha...  2.72 us

profile of v5, /device:TPU:1, one launch (start us, length us, event | category | flops | bytes accessed | tf_op | source)
XLA Modules:
  0.0 84.1 jit_solution(14902931285883923247)
XLA Ops:
  1.3 0.0 copy-start.2
  1.4 0.0 copy-start.3
  1.4 41.8 %conditional.2 = (f32[4,4,2,4,32,128]{5,4,3,2,1,0:T(8,128)S(1)}) conditional(s32[]{:T(128)} %bitcast.8, (f32[2]{0:T(128)}, f32[4,4,2,128,128]{4,3,2,1,0:T(8,128)}, f32[4,4,2,128,128]{4,3,2,1,0:T(8,128)}) %tuple.61, (f32[2]{0:T(128)}, f32[4,4,2,128,128]{4,3,2,1,0:T(8,128)}, ...), branch_computations={%region_0.0_spmd, %region_1.0_spmd, %region_2.0_spmd, %region_3.0_... | conditional | bytes 8 | solution.py:719
  1.4 41.7 %branch_4_fun.1 = f32[4,4,2,4,32,128]{5,4,3,2,1,0:T(8,128)S(1)} custom-call(f32[2]{0:T(128)} %get-tuple-element.74.weight_ref, f32[4,4,2,128,128]{4,3,2,1,0:T(8,128)} %get-tuple-element.75.less_hbm, f32[4,4,2,128,128]{4,3,2,1,0:T(8,128)} %get-tuple-element.76.great_hbm), custom_call_target="tpu_custom_call" | custom-call | tf_op jit(solution)/shard_map/cond/branch_4_fun/pallas_call | solution.py:530
  43.2 0.0 copy-done.2
  43.2 0.0 copy-done.3
  43.2 35.8 %shard_map.85 = (f32[4,4,2,128,128]{4,3,2,1,0:T(8,128)S(1)}, f32[1,1]{1,0:T(1,128)}, s32[1,1]{1,0:T(1,128)}) custom-call(f32[3,4]{1,0:T(4,128)S(1)} %pad_maximum_fusion.scal_ref, f32[4,4,2,4,32,128]{5,4,3,2,1,0:T(8,128)S(1)} %get-tuple-element.127.share_ref, f32[4,2,128,128]{3,2,1,0:T(8,128)S(1)} %bitcast.34, f32[2,128,128]{2,1,0:T(8,128)S(1)} %bitcast.39), custom_call_target="tpu_custom_call" | custom-call | tf_op jit(solution)/shard_map/pallas_call | solution.py:680
  79.6 2.7 %conditional.3 = (f32[4,4,2,128,128]{4,3,2,1,0:T(8,128)}, f32[4,4,2,128,128]{4,3,2,1,0:T(8,128)}, f32[]{:T(128)}) conditional(s32[]{:T(128)} %bitcast.13, (f32[4,4,2,128,128]{4,3,2,1,0:T(8,128)S(1)}, f32[1,1]{1,0:T(1,128)}) %tuple.45, (f32[4,4,2,4,32,128]{5,4,3,2,1,0:T(8,128)S(1)}, f32[3,4]{1,0:T(4,128)S(1)}, f32[4,2,128,128]{3,2,1,0:T(8,128)S(1)}, ...), branch_computations={%region_7.0_spmd, %region_8.11_spmd} | conditional | flops 20001574912 | bytes 45770004 | solution.py:750
  79.6 2.7 %branch_0_fun.3 = (f32[4,4,2,128,128]{4,3,2,1,0:T(8,128)}, f32[4,4,2,128,128]{4,3,2,1,0:T(8,128)}) custom-call(f32[4,4,2,128,128]{4,3,2,1,0:T(8,128)S(1)} %get-tuple-element.83.packed_ref), custom_call_target="tpu_custom_call" | custom-call | tf_op jit(solution)/shard_map/cond/branch_0_fun/pallas_call | solution.py:395
  (3 shorter events, 0.0 us)
Async XLA Ops:
  1.3 41.8 %copy-start.2 = (f32[1,4,2,128,128]{4,3,2,1,0:T(8,128)S(1)}, f32[1,4,2,128,128]{4,3,2,1,0:T(8,128)}, u32[]{:S(2)}) copy-start(f32[1,4,2,128,128]{4,3,2,1,0:T(8,128)} %param.17) | copy-start | bytes 1572868
  1.4 41.8 %copy-start.3 = (f32[1,2,128,128]{3,2,1,0:T(8,128)S(1)}, f32[1,2,128,128]{3,2,1,0:T(8,128)}, u32[]{:S(2)}) copy-start(f32[1,2,128,128]{3,2,1,0:T(8,128)} %param.18) | copy-start | bytes 393220
